TPU v7x, 32 devices: a 4x4x1 block of a 4x4x8 slice. The times are simulated.
32 devices in a mesh: dp: 1 (over z), tp: 4 (over y), ep: 8 (over x, core).
Axes of the slice: x: 4, y: 4, z: 1, core: 2. Of those that a mesh axis runs over, the one named last changes fastest.
The devices are a block of a 4x4x8 slice.
Arguments:
- emb: bfloat16 [2, 256, 2048], P(None, ('dp', 'ep'))
- pos: int32 [256], P(('dp', 'ep'))
- route_ids: int32 [2, 256, 6], P(None, ('dp', 'ep'))
- lat_cache: bfloat16 [2, 256, 128, 512], P(None, ('dp', 'ep'))
- rope_cache: bfloat16 [2, 256, 128, 64], P(None, ('dp', 'ep'))
- attn_norm: float32 [2, 2048], replicated
- w_q: bfloat16 [2, 2048, 16, 192], P(None, None, 'tp')
- w_dkv: bfloat16 [2, 2048, 576], replicated
- kv_norm: float32 [2, 512], replicated
- w_uk: bfloat16 [2, 512, 16, 128], P(None, None, 'tp')
- w_uv: bfloat16 [2, 512, 16, 128], P(None, None, 'tp')
- w_o: bfloat16 [2, 2048, 2048], P(None, 'tp')
- mlp_norm: float32 [2, 2048], replicated
- dense_gate: bfloat16 [2048, 10944], P(None, 'tp')
- dense_up: bfloat16 [2048, 10944], P(None, 'tp')
- dense_down: bfloat16 [10944, 2048], P('tp')
- router: bfloat16 [2048, 64], replicated
- shared_gate: bfloat16 [2048, 2816], P(None, 'tp')
- shared_up: bfloat16 [2048, 2816], P(None, 'tp')
- shared_down: bfloat16 [2816, 2048], P('tp')
- expert_gate: bfloat16 [64, 2048, 1408], P('ep', None, 'tp')
- expert_up: bfloat16 [64, 2048, 1408], P('ep', None, 'tp')
- expert_down: bfloat16 [64, 1408, 2048], P('ep', 'tp')
Outputs:
- output 1: bfloat16 [2, 256, 2048], P(None, ('dp', 'ep'))
- output 2: bfloat16 [2, 256, 128, 512], P(None, ('dp', 'ep'))
- output 3: bfloat16 [2, 256, 128, 64], P(None, ('dp', 'ep'))
All inputs are finite; a program needn't handle non-finite values.
Results may differ from a plain program's by a relative error of at most 0.02.
Values are sent between devices in bfloat16 or wider.
A program may use at most 768 MiB of HBM per device.

v0:
```python
import math
import jax
import jax.numpy as jnp
from jax import lax
from jax.sharding import PartitionSpec as P

NORM_EPS = 1e-6
ROPE_THETA = 10000.0


def rms_norm(values, gain):
    wide = values.astype(jnp.float32)
    mean_sq = jnp.mean(wide * wide, axis=-1, keepdims=True)
    return (wide * lax.rsqrt(mean_sq + NORM_EPS) * gain).astype(jnp.bfloat16)


def rope_tables(position, rope_dim):
    half_dim = rope_dim // 2
    inv_freq = ROPE_THETA ** (-(jnp.arange(half_dim, dtype=jnp.float32) * 2.0 / rope_dim))
    angles = position.astype(jnp.float32)[:, None] * inv_freq[None, :]
    return jnp.cos(angles), jnp.sin(angles)


def rotary(values, cos_t, sin_t):
    wide = values.astype(jnp.float32)
    half_dim = wide.shape[-1] // 2
    first = wide[..., :half_dim]
    second = wide[..., half_dim:]
    return jnp.concatenate([first * cos_t - second * sin_t, second * cos_t + first * sin_t], axis=-1)


def local_attention(hidden, cur_pos, cos_t, sin_t, lat, rop, g_attn, w_query, w_dkv, g_kv, w_uk, w_uv, w_out):
    nope_dim = w_uk.shape[2]
    qk_dim = w_query.shape[2]
    value_a7 = g_kv.shape[0]
    cache_len = lat.shape[1]
    normed = rms_norm(hidden, g_attn)
    query = jnp.einsum('bd,dhk->bhk', normed, w_query, preferred_element_type=jnp.float32)
    q_nope = query[..., :nope_dim].astype(jnp.bfloat16)
    q_rope = rotary(query[..., nope_dim:], cos_t[:, None, :], sin_t[:, None, :]).astype(jnp.bfloat16)
    kv_proj = jnp.dot(normed, w_dkv, preferred_element_type=jnp.float32)
    lat_new = rms_norm(kv_proj[:, :value_a7], g_kv)
    rope_new = rotary(kv_proj[:, value_a7:], cos_t, sin_t).astype(jnp.bfloat16)
    slot_ids = jnp.arange(cache_len)
    hit_mask = (slot_ids[None, :] == cur_pos[:, None])[:, :, None]
    lat = jnp.where(hit_mask, lat_new[:, None, :], lat)
    rop = jnp.where(hit_mask, rope_new[:, None, :], rop)
    q_lat = jnp.einsum('bhn,chn->bhc', q_nope, w_uk, preferred_element_type=jnp.float32).astype(jnp.bfloat16)
    scores = (jnp.einsum('bhc,btc->bht', q_lat, lat, preferred_element_type=jnp.float32) + jnp.einsum('bhr,btr->bht', q_rope, rop, preferred_element_type=jnp.float32)) * (1.0 / math.sqrt(qk_dim))
    visible = slot_ids[None, None, :] <= cur_pos[:, None, None]
    scores = jnp.where(visible, scores, -1e30)
    prob_bf = jax.nn.softmax(scores, axis=-1).astype(jnp.bfloat16)
    o_lat = jnp.einsum('bht,btc->bhc', prob_bf, lat, preferred_element_type=jnp.float32).astype(jnp.bfloat16)
    heads_out = jnp.einsum('bhc,chv->bhv', o_lat, w_uv, preferred_element_type=jnp.float32).astype(jnp.bfloat16)
    attn_part = jnp.dot(heads_out.reshape(hidden.shape[0], -1), w_out, preferred_element_type=jnp.float32)
    return attn_part, lat, rop


def swiglu(normed, w_gate, w_up, w_down):
    gate_h = jnp.dot(normed, w_gate, preferred_element_type=jnp.float32)
    up_h = jnp.dot(normed, w_up, preferred_element_type=jnp.float32)
    act_bf = (jax.nn.silu(gate_h) * up_h).astype(jnp.bfloat16)
    return jnp.dot(act_bf, w_down, preferred_element_type=jnp.float32)


def routed_local(normed, expert_ids, router, expert_gate, expert_up, expert_down):
    logits = jnp.dot(normed, router, preferred_element_type=jnp.float32)
    route_w = jnp.take_along_axis(jax.nn.softmax(logits, axis=-1), expert_ids, axis=1)
    tok_all = lax.all_gather(normed, 'ep', axis=0, tiled=True)
    ids_all = lax.all_gather(expert_ids, 'ep', axis=0, tiled=True)
    weight_all = lax.all_gather(route_w, 'ep', axis=0, tiled=True)
    local_count = expert_gate.shape[0]
    top_k = expert_ids.shape[1]
    flat_ids = ids_all.reshape(-1) - lax.axis_index('ep') * local_count
    in_range = (flat_ids >= 0) & (flat_ids < local_count)
    sort_key = jnp.where(in_range, flat_ids, local_count)
    sort_order = jnp.argsort(sort_key, stable=True)
    group_sizes = jnp.sum((sort_key[:, None] == jnp.arange(local_count)[None, :]).astype(jnp.int32), axis=0)
    tok_index = sort_order // top_k
    sorted_rows = jnp.take(tok_all, tok_index, axis=0)
    gate_h = lax.ragged_dot(sorted_rows, expert_gate, group_sizes, preferred_element_type=jnp.float32)
    up_h = lax.ragged_dot(sorted_rows, expert_up, group_sizes, preferred_element_type=jnp.float32)
    act_bf = (jax.nn.silu(gate_h) * up_h).astype(jnp.bfloat16)
    down = lax.ragged_dot(act_bf, expert_down, group_sizes, preferred_element_type=jnp.float32)
    keep_mask = in_range[sort_order]
    sorted_w = weight_all.reshape(-1)[sort_order]
    contrib = jnp.where(keep_mask[:, None], down * sorted_w[:, None], 0.0)
    token_sum = jax.ops.segment_sum(contrib, tok_index, num_segments=tok_all.shape[0])
    return lax.psum_scatter(token_sum, 'ep', scatter_dimension=0, tiled=True)


def solution(mesh):
    tok_axes = ('dp', 'ep')

    def device_fn(emb, pos, route_ids, lat_cache, rope_cache, attn_norm, w_q, w_dkv, kv_norm, w_uk, w_uv, w_o, mlp_norm, dense_gate, dense_up, dense_down, router, shared_gate, shared_up, shared_down, expert_gate, expert_up, expert_down):
        lat_first, lat_second = lat_cache[0], lat_cache[1]
        rop_first, rop_second = rope_cache[0], rope_cache[1]
        hidden_steps = []
        for step_idx in range(2):
            cur_pos = pos + step_idx
            cos_t, sin_t = rope_tables(cur_pos, rope_cache.shape[-1])
            attn_part, lat_first, rop_first = local_attention(emb[step_idx], cur_pos, cos_t, sin_t, lat_first, rop_first, attn_norm[0], w_q[0], w_dkv[0], kv_norm[0], w_uk[0], w_uv[0], w_o[0])
            y_first = (emb[step_idx].astype(jnp.float32) + lax.psum(attn_part, 'tp')).astype(jnp.bfloat16)
            dense_part = swiglu(rms_norm(y_first, mlp_norm[0]), dense_gate, dense_up, dense_down)
            h_mid = (y_first.astype(jnp.float32) + lax.psum(dense_part, 'tp')).astype(jnp.bfloat16)
            attn_part, lat_second, rop_second = local_attention(h_mid, cur_pos, cos_t, sin_t, lat_second, rop_second, attn_norm[1], w_q[1], w_dkv[1], kv_norm[1], w_uk[1], w_uv[1], w_o[1])
            y_second = (h_mid.astype(jnp.float32) + lax.psum(attn_part, 'tp')).astype(jnp.bfloat16)
            normed = rms_norm(y_second, mlp_norm[1])
            routed_part = routed_local(normed, route_ids[step_idx], router, expert_gate, expert_up, expert_down)
            moe_sum = lax.psum(routed_part + swiglu(normed, shared_gate, shared_up, shared_down), 'tp')
            hidden_steps.append((y_second.astype(jnp.float32) + moe_sum).astype(jnp.bfloat16))
        return jnp.stack(hidden_steps), jnp.stack([lat_first, lat_second]), jnp.stack([rop_first, rop_second])

    in_specs = (P(None, tok_axes, None), P(tok_axes), P(None, tok_axes, None), P(None, tok_axes, None, None), P(None, tok_axes, None, None), P(), P(None, None, 'tp', None), P(), P(), P(None, None, 'tp', None), P(None, None, 'tp', None), P(None, 'tp', None), P(), P(None, 'tp'), P(None, 'tp'), P('tp', None), P(), P(None, 'tp'), P(None, 'tp'), P('tp', None), P('ep', None, 'tp'), P('ep', None, 'tp'), P('ep', 'tp', None))
    out_specs = (P(None, tok_axes, None), P(None, tok_axes, None, None), P(None, tok_axes, None, None))
    return jax.shard_map(device_fn, mesh=mesh, in_specs=in_specs, out_specs=out_specs, check_vma=False)
```

profile of v0, /device:TPU:96, one launch (start us, length us, event | category | flops | bytes accessed | tf_op | source)
XLA Modules:
  0.0 624.6 jit_solution(2074571461190799600)
XLA Ops:
  9.9 2.7 fusion.38
  12.6 2.7 fusion.40
  15.4 3.1 fusion.28
  26.6 2.6 fusion.63
  29.2 2.8 fusion.275
  32.0 3.1 fusion.67
  36.3 3.8 fusion.17
  40.1 2.5 fusion.274
  42.6 3.3 fusion.69
  49.4 23.1 %all-gather = s32[1,256,6]{2,0,1:T(1,128)S(1)} all-gather(s32[1,32,6]{2,0,1:T(1,128)} %copy.107), channel_id=2, replica_groups=mesh['dp'=1,'tp'=4,'ep'=8] {'ep'}, dimensions={1}, use_global_device_ids=true | all-gather | bytes 6912 | tf_op jit(solution)/shard_map/all_gather | solution.py:70
  73.2 22.0 %all-gather.1 = s32[1,256,6]{2,0,1:T(1,128)} all-gather(s32[1,32,6]{2,0,1:T(1,128)} %copy.122), channel_id=3, replica_groups=mesh['dp'=1,'tp'=4,'ep'=8] {'ep'}, dimensions={1}, use_global_device_ids=true | all-gather | bytes 6912 | tf_op jit(solution)/shard_map/all_gather | solution.py:70
  95.2 2.4 subtract_reduce_fusion
  102.1 8.4 %fusion.196 = f32[32,2736]{1,0:T(8,128)} fusion(bf16[2048,2736]{0,1:T(8,128)(2,1)} %param.40, bf16[32,2048]{1,0:T(8,128)(2,1)S(1)} %get-tuple-element.56, f32[2048]{0:T(1024)S(1)} %bitcast.228, f32[32]{0:T(128)S(1)} %add_rsqrt_fusion.9), kind=kOutput, calls=%fused_computation.288 | convolution fusion | flops 358875136 | bytes 11696256 | tf_op jit(solution)/shard_map/dot_general | solution.py:60
  110.5 8.4 %fusion.190 = f32[32,2736]{1,0:T(8,128)} fusion(bf16[2048,2736]{0,1:T(8,128)(2,1)} %param.40, bf16[32,2048]{1,0:T(8,128)(2,1)S(1)} %get-tuple-element.68, f32[32]{0:T(128)S(1)} %add_rsqrt_fusion.3, f32[2048]{0:T(1024)S(1)} %bitcast.229), kind=kOutput, calls=%fused_computation.287 | convolution fusion | flops 358875136 | bytes 11696256 | tf_op jit(solution)/shard_map/dot_general | solution.py:60
  118.8 13.6 %fusion.99 = f32[32,2048]{1,0:T(8,128)} fusion(bf16[2736,2048]{1,0:T(8,128)(2,1)} %param.42, bf16[2048,2736]{0,1:T(8,128)(2,1)} %param.41, f32[32,2736]{1,0:T(8,128)} %fusion.196, bf16[32,2048]{1,0:T(8,128)(2,1)} %copy-done.7, f32[2048]{0:T(1024)S(1)} %bitcast.230, f32[32]{0:T(128)} %copy-done.76), kind=kOutput, calls=%fused_computation.139 | convolution fusion | flops 718013440 | bytes 23165056 | tf_op jit(solution)/shard_map/dot_general | solution.py:63
  132.5 13.7 %fusion.98 = f32[32,2048]{1,0:T(8,128)} fusion(bf16[2736,2048]{1,0:T(8,128)(2,1)} %param.42, bf16[2048,2736]{0,1:T(8,128)(2,1)} %param.41, f32[32,2736]{1,0:T(8,128)} %fusion.190, bf16[32,2048]{1,0:T(8,128)(2,1)S(1)} %get-tuple-element.68, f32[32]{0:T(128)} %copy-done.75, f32[2048]{0:T(1024)S(1)} %bitcast.231), kind=kOutput, calls=%fused_computation.138 | convolution fusion | flops 718013440 | bytes 23165056 | tf_op jit(solution)/shard_map/dot_general | solution.py:63
  148.6 5.7 sort.31
  155.7 30.5 %all-reduce.13.cloned.1.call-done = (f32[32,2048]{1,0:T(8,128)}, f32[32,2048]{1,0:T(8,128)}) async-done(((f32[32,2048]{1,0:T(8,128)}, f32[32,2048]{1,0:T(8,128)}), (f32[32,2048]{1,0:T(8,128)}, f32[32,2048]{1,0:T(8,128)})) %all-reduce.13.cloned.1.call-update) | async-done | bytes 524304 | tf_op jit(solution)/shard_map/psum | solution.py:105
  187.4 3.2 fusion.24
  190.6 2.5 fusion.36
  193.3 2.6 fusion.34
  196.4 3.0 fusion.22
  201.1 1.9 fusion.65
  203.1 1.7 fusion.277
  204.8 2.9 fusion.66
  209.8 3.2 fusion.19
  213.0 1.9 fusion.276
  214.9 3.3 fusion.68
  220.5 37.9 %all-reduce.11.cloned.1.call-done = (f32[32,2048]{1,0:T(8,128)}, f32[32,2048]{1,0:T(8,128)}) async-done(((f32[32,2048]{1,0:T(8,128)}, f32[32,2048]{1,0:T(8,128)}), (f32[32,2048]{1,0:T(8,128)}, f32[32,2048]{1,0:T(8,128)})) %all-reduce.11.cloned.1.call-update) | async-done | bytes 524304 | tf_op jit(solution)/shard_map/psum | solution.py:107
  262.3 1.5 ragged-dot-metadata.1
  263.9 15.4 %copy.108 = bf16[8,2048,352]{2,1,0:T(8,128)(2,1)} copy(bf16[8,2048,352]{1,2,0:T(8,128)(2,1)} %param.47) | data formatting | bytes 23068672 | tf_op args[20]
  279.3 15.4 %copy.109 = bf16[8,2048,352]{2,1,0:T(8,128)(2,1)} copy(bf16[8,2048,352]{1,2,0:T(8,128)(2,1)} %param.48) | data formatting | bytes 23068672 | tf_op args[21]
  294.9 5.0 sort.32
  301.7 12.8 %gather_fusion = pred[1536]{0:T(1024)(128)(4,1)} fusion(pred[1536]{0:T(1024)(128)(4,1)S(1)} %compare_and_fusion.3, s32[2048]{0:T(1024)S(1)} %pad_clamp_fusion.3), kind=kCustom, calls=%fused_computation.4 | custom fusion | bytes 9216 | tf_op jit(solution)/shard_map/gather | solution.py:85
  316.8 1.6 gather_fusion.5
  318.6 23.6 %all-gather.2 = f32[8,32,6]{1,2,0:T(8,128)S(1)} all-gather(f32[1,32,6]{1,2,0:T(8,128)S(1)} %select_bitcast_fusion.1), channel_id=1, replica_groups=mesh['dp'=1,'tp'=4,'ep'=8] {'ep'}, dimensions={0}, use_global_device_ids=true | all-gather | bytes 6912 | tf_op jit(solution)/shard_map/all_gather | solution.py:71
  342.4 8.4 %gather_fusion.1 = f32[1536]{0:T(1024)S(1)} fusion(f32[1536]{0:T(1024)S(1)} %reshape.479, s32[2048]{0:T(1024)S(1)} %pad_clamp_fusion.3), kind=kCustom, calls=%fused_computation.5 | custom fusion | bytes 18432 | tf_op jit(solution)/shard_map/gather | solution.py:86
  351.0 14.0 %gather_fusion.4 = bf16[1536,2048]{1,0:T(8,128)(2,1)} fusion(bf16[256,2048]{1,0:T(8,128)(2,1)} %all-gather.7.cloned.1.call-done, s32[2048]{0:T(1024)S(1)} %pad_clamp_fusion.2), kind=kCustom, calls=%fused_computation.clone | custom fusion | bytes 12589056 | tf_op jit(solution)/shard_map/jit(_take)/gather | solution.py:80
  365.1 6.1 broadcast_select_fusion.1
  371.2 5.0 ragged-dot-none.5
  376.2 5.0 ragged-dot-none.4
  381.2 4.0 multiply_convert_fusion.1
  385.3 5.5 ragged-dot-none.3
  390.8 23.6 %scatter_custom_fusion = f32[256,2048]{1,0:T(8,128)} fusion(s32[1536]{0:T(1024)S(1)} %get-tuple-element.44, f32[1536,2048]{1,0:T(8,128)} %ragged-dot-none.3, f32[]{:T(128)} %constant.45.clone.1, f32[1536]{0:T(1024)S(1)} %gather_fusion.1, pred[1536]{0:T(1024)(128)(4,1)S(1)} %copy-done.62), kind=kCustom, calls=%fused_computation.17 | custom fusion | flops 9437184 | bytes 14691328 | tf_op jit(solution)/shard_map/scatter-add | solution.py:88
  414.6 9.5 %gather_fusion.2 = pred[1536]{0:T(1024)(128)(4,1)S(1)} fusion(pred[1536]{0:T(1024)(128)(4,1)S(1)} %compare_and_fusion.2, s32[2048]{0:T(1024)S(1)} %pad_clamp_fusion.1), kind=kCustom, calls=%fused_computation.6 | custom fusion | bytes 9216 | tf_op jit(solution)/shard_map/gather | solution.py:85
  425.7 1.6 gather_fusion.7
  427.5 29.2 %all-gather.3 = f32[8,32,6]{1,2,0:T(8,128)S(1)} all-gather(f32[1,32,6]{1,2,0:T(8,128)S(1)} %select_bitcast_fusion), channel_id=1, replica_groups=mesh['dp'=1,'tp'=4,'ep'=8] {'ep'}, dimensions={0}, use_global_device_ids=true | all-gather | bytes 6912 | tf_op jit(solution)/shard_map/all_gather | solution.py:71
  458.5 8.4 %gather_fusion.3 = f32[1536]{0:T(1024)S(1)} fusion(f32[1536]{0:T(1024)S(1)} %reshape.482, s32[2048]{0:T(1024)S(1)} %pad_clamp_fusion.1), kind=kCustom, calls=%fused_computation.7 | custom fusion | bytes 18432 | tf_op jit(solution)/shard_map/gather | solution.py:86
  466.9 14.0 %gather_fusion.6 = bf16[1536,2048]{1,0:T(8,128)(2,1)} fusion(bf16[256,2048]{1,0:T(8,128)(2,1)} %all-gather.9.cloned.1.call-done, s32[2048]{0:T(1024)S(1)} %pad_clamp_fusion), kind=kCustom, calls=%fused_computation.2.clone | custom fusion | bytes 12589056 | tf_op jit(solution)/shard_map/jit(_take)/gather | solution.py:80
  480.9 6.1 broadcast_select_fusion
  487.1 5.4 ragged-dot-none.2
  492.4 5.2 ragged-dot-none.1
  497.6 4.0 multiply_convert_fusion
  501.6 5.5 ragged-dot-none
  507.2 23.7 %scatter_custom_fusion.1 = f32[256,2048]{1,0:T(8,128)} fusion(s32[1536]{0:T(1024)S(1)} %get-tuple-element.48, f32[1536,2048]{1,0:T(8,128)} %ragged-dot-none, f32[1536]{0:T(1024)S(1)} %gather_fusion.3, f32[]{:T(128)} %constant.45.clone.1, pred[1536]{0:T(1024)(128)(4,1)S(1)} %gather_fusion.2), kind=kCustom, calls=%fused_computation.14 | custom fusion | flops 9437184 | bytes 14691328 | tf_op jit(solution)/shard_map/scatter-add | solution.py:88
  531.3 3.1 select_select_fusion.3
  534.4 7.7 %select_select_fusion.1 = (bf16[1,32,128,512]{3,2,1,0:T(8,128)(2,1)}, bf16[1,32,128,512]{3,2,1,0:T(8,128)(2,1)}) fusion(pred[32,128]{1,0:T(8,128)(4,1)S(1)} %copy-done.47, pred[32,128]{1,0:T(8,128)(4,1)S(1)} %copy-done.44, bf16[2,32,128,512]{3,2,1,0:T(8,128)(2,1)} %param.30, bf16[32,512]{1,0:T(8,128)(2,1)S(1)} %copy-done.31, ...), kind=kLoop, calls=%fused_computation.32 | loop fusion | flops 8388608 | bytes 16916480 | tf_op jit(solution)/shard_map/jit(_where)/select_n | solution.py:46
  542.1 1.6 fusion.292
  544.6 4.3 convolution_add_fusion.1
  549.0 24.4 %reduce-scatter.5.cloned.1.call-done = f32[32,2048]{1,0:T(8,128)} async-done(((f32[256,2048]{1,0:T(8,128)}), f32[32,2048]{1,0:T(8,128)}) %reduce-scatter.5.cloned.1.call-update) | async-done | bytes 262160 | tf_op jit(solution)/shard_map/reduce_scatter | solution.py:89
  573.4 4.3 convolution_add_fusion
  577.7 2.3 pad_maximum_fusion.1
  580.0 7.6 %pad_maximum_fusion = bf16[2,32,128,512]{3,2,1,0:T(8,128)(2,1)} fusion(bf16[1,32,128,512]{3,2,1,0:T(8,128)(2,1)} %get-tuple-element.60, bf16[1,32,128,512]{3,2,1,0:T(8,128)(2,1)} %get-tuple-element.59), kind=kLoop, calls=%fused_computation.20 | loop fusion | flops 4194304 | bytes 16777216 | tf_op jit(solution)/shard_map/stack | solution.py:112
  587.6 27.0 %all-reduce.9.cloned.1.call-done = (f32[32,2048]{1,0:T(8,128)}, f32[32,2048]{1,0:T(8,128)}) async-done(((f32[32,2048]{1,0:T(8,128)}, f32[32,2048]{1,0:T(8,128)}), (f32[32,2048]{1,0:T(8,128)}, f32[32,2048]{1,0:T(8,128)})) %all-reduce.9.cloned.1.call-update) | async-done | bytes 524304 | tf_op jit(solution)/shard_map/psum | solution.py:110
  (301 shorter events, 48.3 us)
Async XLA Ops:
  7.2 537.4 %copy-start = (bf16[704,2048]{1,0:T(8,128)(2,1)S(1)}, bf16[704,2048]{1,0:T(8,128)(2,1)}, u32[]{:S(2)}) copy-start(bf16[704,2048]{1,0:T(8,128)(2,1)} %param.46) | copy-start | bytes 8650756
  7.2 8.1 %copy-start.8 = (bf16[2,32,2048]{2,1,0:T(8,128)(2,1)S(1)}, bf16[2,32,2048]{2,1,0:T(8,128)(2,1)}, u32[]{:S(2)}) copy-start(bf16[2,32,2048]{2,1,0:T(8,128)(2,1)} %param.27) | copy-start | bytes 786436
  7.2 93.4 %all-reduce.15.cloned.1.call-start = ((), (), s32[]{:S(2)}) async-start(), calls=%async_computation.9 | async-start | bytes 1048576 | tf_op jit(solution)/shard_map/psum | solution.py:103
  7.3 16.9 %copy-start.77 = (f32[32]{0:T(128)}, f32[32]{0:T(128)S(1)}, u32[]{:S(2)}) copy-start(f32[32]{0:T(128)S(1)} %negate_power_fusion) | copy-start | bytes 388
  9.9 8.6 %copy-start.80 = (bf16[2,2048,4,192]{1,3,2,0:T(8,128)(2,1)S(1)}, bf16[2,2048,4,192]{1,3,2,0:T(8,128)(2,1)}, u32[]{:S(2)}) copy-start(bf16[2,2048,4,192]{1,3,2,0:T(8,128)(2,1)} %param.33) | copy-start | bytes 18874372
  12.6 13.9 %slice-start = ((s8[8388608]{0:T(1024)(128)(4,1)}), s8[4194304]{0:T(1024)(128)(4,1)S(1)}, s32[]{:S(2)}) async-start(s8[8388608]{0:T(1024)(128)(4,1)} %bitcast.224), calls=%async_computation.10 | async-start | bytes 8388608
  15.3 4.6 copy-start.74
  15.3 5.9 copy-start.9
  15.3 6.2 copy-start.10
  18.5 8.0 %slice-start.1 = ((s8[8388608]{0:T(1024)(128)(4,1)}), s8[4194304]{0:T(1024)(128)(4,1)S(1)}, s32[]{:S(2)}) async-start(s8[8388608]{0:T(1024)(128)(4,1)} %bitcast.224), calls=%async_computation.11 | async-start | bytes 8388608
  19.6 6.2 copy-start.67
  19.7 6.2 copy-start.69
  21.2 21.3 %copy-start.42 = (pred[32,128]{1,0:T(8,128)(4,1)}, pred[32,128]{1,0:T(8,128)(4,1)S(1)}, u32[]{:S(2)}) copy-start(pred[32,128]{1,0:T(8,128)(4,1)S(1)} %get-tuple-element.110) | copy-start | bytes 12292
  21.2 21.3 %copy-start.45 = (pred[32,128]{1,0:T(8,128)(4,1)}, pred[32,128]{1,0:T(8,128)(4,1)S(1)}, u32[]{:S(2)}) copy-start(pred[32,128]{1,0:T(8,128)(4,1)S(1)} %get-tuple-element.134) | copy-start | bytes 12292
  25.8 14.2 %copy-start.49 = (bf16[32,64]{1,0:T(8,128)(2,1)}, bf16[32,64]{1,0:T(8,128)(2,1)S(1)}, u32[]{:S(2)}) copy-start(bf16[32,64]{1,0:T(8,128)(2,1)S(1)} %pad_maximum_fusion.7) | copy-start | bytes 12292
  36.2 6.3 %copy-start.30 = (bf16[32,512]{1,0:T(8,128)(2,1)S(1)}, bf16[32,512]{1,0:T(8,128)(2,1)}, u32[]{:S(2)}) copy-start(bf16[32,512]{1,0:T(8,128)(2,1)} %copy-done.28) | copy-start | bytes 98308
  36.2 6.3 %copy-start.33 = (bf16[32,512]{1,0:T(8,128)(2,1)S(1)}, bf16[32,512]{1,0:T(8,128)(2,1)}, u32[]{:S(2)}) copy-start(bf16[32,512]{1,0:T(8,128)(2,1)} %get-tuple-element.98) | copy-start | bytes 98308
  48.6 137.6 %all-reduce.13.cloned.1.call-start = ((), (), s32[]{:S(2)}) async-start(), calls=%async_computation.8 | async-start | bytes 1048576 | tf_op jit(solution)/shard_map/psum | solution.py:105
  48.7 97.6 %copy-start.40 = (s32[1,32,6]{1,0,2:T(1,128)}, s32[1,32,6]{1,0,2:T(1,128)S(1)}, u32[]{:S(2)}) copy-start(s32[1,32,6]{1,0,2:T(1,128)S(1)} %get-tuple-element.91) | copy-start | bytes 2308
  102.0 8.5 %copy-start.7 = (bf16[32,2048]{1,0:T(8,128)(2,1)}, bf16[32,2048]{1,0:T(8,128)(2,1)S(1)}, u32[]{:S(2)}) copy-start(bf16[32,2048]{1,0:T(8,128)(2,1)S(1)} %get-tuple-element.56) | copy-start | bytes 393220
  102.0 8.4 %copy-start.76 = (f32[32]{0:T(128)}, f32[32]{0:T(128)S(1)}, u32[]{:S(2)}) copy-start(f32[32]{0:T(128)S(1)} %add_rsqrt_fusion.9) | copy-start | bytes 388
  102.0 8.4 %copy-start.75 = (f32[32]{0:T(128)}, f32[32]{0:T(128)S(1)}, u32[]{:S(2)}) copy-start(f32[32]{0:T(128)S(1)} %add_rsqrt_fusion.3) | copy-start | bytes 388
  146.3 112.1 %all-reduce.11.cloned.1.call-start = ((), (), s32[]{:S(2)}) async-start(), calls=%async_computation.7 | async-start | bytes 1048576 | tf_op jit(solution)/shard_map/psum | solution.py:107
  186.2 4.4 copy-start.64
  186.2 6.9 %copy-start.19 = (f32[32,2048]{1,0:T(8,128)S(1)}, f32[32,2048]{1,0:T(8,128)}, u32[]{:S(2)}) copy-start(f32[32,2048]{1,0:T(8,128)} %get-tuple-element.39) | copy-start | bytes 786436
  187.4 8.6 %copy-start.11 = (bf16[32,2048]{1,0:T(8,128)(2,1)}, bf16[32,2048]{1,0:T(8,128)(2,1)S(1)}, u32[]{:S(2)}) copy-start(bf16[32,2048]{1,0:T(8,128)(2,1)S(1)} %get-tuple-element.52) | copy-start | bytes 393220
  187.4 8.8 %copy-start.68 = (f32[32]{0:T(128)S(1)}, f32[32]{0:T(128)}, u32[]{:S(2)}) copy-start(f32[32]{0:T(128)} %copy-done.67) | copy-start | bytes 388
  187.4 8.8 %copy-start.70 = (f32[32]{0:T(128)S(1)}, f32[32]{0:T(128)}, u32[]{:S(2)}) copy-start(f32[32]{0:T(128)} %copy-done.69) | copy-start | bytes 388
  187.4 8.8 %copy-start.78 = (f32[32]{0:T(128)S(1)}, f32[32]{0:T(128)}, u32[]{:S(2)}) copy-start(f32[32]{0:T(128)} %copy-done.77) | copy-start | bytes 388
  187.4 13.7 %slice-start.2 = ((s8[8388608]{0:T(1024)(128)(4,1)}), s8[4194304]{0:T(1024)(128)(4,1)S(1)}, s32[]{:S(2)}) async-start(s8[8388608]{0:T(1024)(128)(4,1)} %bitcast.226), calls=%async_computation.12 | async-start | bytes 8388608
  193.1 6.3 %copy-start.25 = (f32[32,32]{1,0:T(8,128)S(1)}, f32[32,32]{1,0:T(8,128)}, u32[]{:S(2)}) copy-start(f32[32,32]{1,0:T(8,128)} %copy-done.24) | copy-start | bytes 12292
  193.1 6.3 %copy-start.27 = (f32[32,32]{1,0:T(8,128)S(1)}, f32[32,32]{1,0:T(8,128)}, u32[]{:S(2)}) copy-start(f32[32,32]{1,0:T(8,128)} %copy-done.26) | copy-start | bytes 12292
  193.1 6.7 %copy-start.21 = (f32[32,32]{1,0:T(8,128)S(1)}, f32[32,32]{1,0:T(8,128)}, u32[]{:S(2)}) copy-start(f32[32,32]{1,0:T(8,128)} %get-tuple-element.101) | copy-start | bytes 12292
  193.1 6.7 %copy-start.23 = (f32[32,32]{1,0:T(8,128)S(1)}, f32[32,32]{1,0:T(8,128)}, u32[]{:S(2)}) copy-start(f32[32,32]{1,0:T(8,128)} %get-tuple-element.102) | copy-start | bytes 12292
  193.3 7.6 %copy-start.13 = (bf16[32,2048]{1,0:T(8,128)(2,1)}, bf16[32,2048]{1,0:T(8,128)(2,1)S(1)}, u32[]{:S(2)}) copy-start(bf16[32,2048]{1,0:T(8,128)(2,1)S(1)} %get-tuple-element.54) | copy-start | bytes 393220
  193.3 7.7 %copy-start.63 = (f32[1,512]{1,0:T(1,128)S(1)}, f32[1,512]{1,0:T(1,128)}, u32[]{:S(2)}) copy-start(f32[1,512]{1,0:T(1,128)} %get-tuple-element.93) | copy-start | bytes 6148
  193.3 7.8 %slice-start.3 = ((s8[8388608]{0:T(1024)(128)(4,1)}), s8[4194304]{0:T(1024)(128)(4,1)S(1)}, s32[]{:S(2)}) async-start(s8[8388608]{0:T(1024)(128)(4,1)} %bitcast.226), calls=%async_computation.13 | async-start | bytes 8388608
  193.3 7.8 %copy-start.46 = (pred[32,128]{1,0:T(8,128)(4,1)S(1)}, pred[32,128]{1,0:T(8,128)(4,1)}, u32[]{:S(2)}) copy-start(pred[32,128]{1,0:T(8,128)(4,1)} %copy-done.45) | copy-start | bytes 12292
  201.1 13.8 %copy-start.35 = (bf16[32,512]{1,0:T(8,128)(2,1)}, bf16[32,512]{1,0:T(8,128)(2,1)S(1)}, u32[]{:S(2)}) copy-start(bf16[32,512]{1,0:T(8,128)(2,1)S(1)} %get-tuple-element.96) | copy-start | bytes 98308
  203.1 9.9 %copy-start.53 = (bf16[32,64]{1,0:T(8,128)(2,1)}, bf16[32,64]{1,0:T(8,128)(2,1)S(1)}, u32[]{:S(2)}) copy-start(bf16[32,64]{1,0:T(8,128)(2,1)S(1)} %pad_maximum_fusion.8) | copy-start | bytes 12292
  204.8 5.0 copy-start.37
  204.8 5.0 copy-start.43
  214.9 4.9 copy-start.39
  214.9 5.6 copy-start.59
  214.9 43.5 %copy-start.14 = (bf16[32,2048]{1,0:T(8,128)(2,1)S(1)}, bf16[32,2048]{1,0:T(8,128)(2,1)}, u32[]{:S(2)}) copy-start(bf16[32,2048]{1,0:T(8,128)(2,1)} %copy-done.13) | copy-start | bytes 393220
  218.2 41.3 %copy-start.12 = (bf16[32,2048]{1,0:T(8,128)(2,1)S(1)}, bf16[32,2048]{1,0:T(8,128)(2,1)}, u32[]{:S(2)}) copy-start(bf16[32,2048]{1,0:T(8,128)(2,1)} %copy-done.11) | copy-start | bytes 393220
  218.2 42.4 %copy-start.56 = (f32[1,2048]{1,0:T(1,128)S(1)}, f32[1,2048]{1,0:T(1,128)}, u32[]{:S(2)}) copy-start(f32[1,2048]{1,0:T(1,128)} %get-tuple-element.85) | copy-start | bytes 24580
  219.8 131.2 %all-gather.7.cloned.1.call-start = ((), (), s32[]{:S(2)}) async-start(), calls=%async_computation.2 | async-start | bytes 1179648 | tf_op jit(solution)/shard_map/all_gather | solution.py:69
  261.6 205.3 %all-gather.9.cloned.1.call-start = ((), (), s32[]{:S(2)}) async-start(), calls=%async_computation.4 | async-start | bytes 1179648 | tf_op jit(solution)/shard_map/all_gather | solution.py:69
  279.3 15.5 %copy-start.61 = (s32[32,6,1]{0,1,2:T(8,128)S(1)}, s32[32,6,1]{0,1,2:T(8,128)}, u32[]{:S(2)}) copy-start(s32[32,6,1]{0,1,2:T(8,128)} %bitcast_or_fusion.1) | copy-start | bytes 2308
  279.3 22.2 %copy-start.60 = (s32[32,6,1]{0,1,2:T(8,128)S(1)}, s32[32,6,1]{0,1,2:T(8,128)}, u32[]{:S(2)}) copy-start(s32[32,6,1]{0,1,2:T(8,128)} %bitcast_or_fusion) | copy-start | bytes 2308
  279.3 35.9 %copy-start.6 = (bf16[32,2048]{1,0:T(8,128)(2,1)S(1)}, bf16[32,2048]{1,0:T(8,128)(2,1)}, u32[]{:S(2)}) copy-start(bf16[32,2048]{1,0:T(8,128)(2,1)} %get-tuple-element.89) | copy-start | bytes 393220
  350.9 14.2 %copy-start.65 = (pred[1536]{0:T(1024)(128)(4,1)S(1)}, pred[1536]{0:T(1024)(128)(4,1)}, u32[]{:S(2)}) copy-start(pred[1536]{0:T(1024)(128)(4,1)} %get-tuple-element.43) | copy-start | bytes 4612
  350.9 193.7 %reduce-scatter.3.cloned.1.call-start = ((), (), s32[]{:S(2)}) async-start(), calls=%async_computation.3 | async-start | bytes 2359296 | tf_op jit(solution)/shard_map/reduce_scatter | solution.py:89
  385.3 5.5 copy-start.62
  414.5 9.7 %copy-start.5 = (bf16[32,2048]{1,0:T(8,128)(2,1)S(1)}, bf16[32,2048]{1,0:T(8,128)(2,1)}, u32[]{:S(2)}) copy-start(bf16[32,2048]{1,0:T(8,128)(2,1)} %get-tuple-element.90) | copy-start | bytes 393220
  414.5 158.8 %reduce-scatter.5.cloned.1.call-start = ((), (), s32[]{:S(2)}) async-start(), calls=%async_computation.5 | async-start | bytes 2359296 | tf_op jit(solution)/shard_map/reduce_scatter | solution.py:89
  507.1 24.1 %copy-start.44 = (pred[32,128]{1,0:T(8,128)(4,1)S(1)}, pred[32,128]{1,0:T(8,128)(4,1)}, u32[]{:S(2)}) copy-start(pred[32,128]{1,0:T(8,128)(4,1)} %copy-done.42) | copy-start | bytes 12292
  507.1 24.1 %copy-start.47 = (pred[32,128]{1,0:T(8,128)(4,1)S(1)}, pred[32,128]{1,0:T(8,128)(4,1)}, u32[]{:S(2)}) copy-start(pred[32,128]{1,0:T(8,128)(4,1)} %copy-done.45) | copy-start | bytes 12292
  507.1 24.1 %copy-start.50 = (bf16[32,64]{1,0:T(8,128)(2,1)S(1)}, bf16[32,64]{1,0:T(8,128)(2,1)}, u32[]{:S(2)}) copy-start(bf16[32,64]{1,0:T(8,128)(2,1)} %copy-done.49) | copy-start | bytes 12292
  507.1 24.1 %copy-start.52 = (bf16[32,64]{1,0:T(8,128)(2,1)S(1)}, bf16[32,64]{1,0:T(8,128)(2,1)}, u32[]{:S(2)}) copy-start(bf16[32,64]{1,0:T(8,128)(2,1)} %copy-done.51) | copy-start | bytes 12292
  507.1 24.1 %copy-start.54 = (bf16[32,64]{1,0:T(8,128)(2,1)S(1)}, bf16[32,64]{1,0:T(8,128)(2,1)}, u32[]{:S(2)}) copy-start(bf16[32,64]{1,0:T(8,128)(2,1)} %copy-done.53) | copy-start | bytes 12292
  530.9 83.7 %all-reduce.9.cloned.1.call-start = ((), (), s32[]{:S(2)}) async-start(), calls=%async_computation.6 | async-start | bytes 1048576 | tf_op jit(solution)/shard_map/psum | solution.py:110
  534.4 7.7 %copy-start.4 = (bf16[2048,704]{0,1:T(8,128)(2,1)S(1)}, bf16[2048,704]{0,1:T(8,128)(2,1)}, u32[]{:S(2)}) copy-start(bf16[2048,704]{0,1:T(8,128)(2,1)} %param.44) | copy-start | bytes 8650756
  (29 other events, 95.8 us)
Sparse Core Ops, SparseCore 0:
  48.8 40.5 all-reduce.14
  146.4 39.7 all-reduce.12
  219.9 38.4 all-reduce.10
  261.7 21.0 all-gather.6
  351.0 19.5 all-gather.8
  414.6 39.3 reduce-scatter.2
  531.0 42.2 reduce-scatter.4
  577.8 36.7 all-reduce.8
where the time goes:
time: 635 us; the launch traced here: 625 us
  other arithmetic  121 us (19%)
  matrix products  120 us (19%)
  waiting for transfers between devices  120 us (19%)
  local copies, waits for them, and re-layouts  114 us (18%)
  blocking collectives  97.8 us (15%)
  Pallas kernels  34.6 us (5%)
  between operations  15.8 us (2%)
    all_gather x2, blocking collectives, routed_local(): weight_all = lax.all_gather(route_w, 'ep', axis=0, tiled=True)  52.7 us
    scatter-add x2, other arithmetic, routed_local(): jax.ops.segment_sum(contrib, tok_index, num_segments=tok_all.shape[0])  47.3 us
    all_gather x2, blocking collectives, routed_local(): ids_all = lax.all_gather(expert_ids, 'ep', axis=0, tiled=True)  45.1 us
    psum x2, waiting for transfers between devices, device_fn(): lax.psum(attn_part, 'tp')  37.9 us
    dot_general x4, matrix products, swiglu(): return jnp.dot(act_bf, w_down, preferred_element_type=jnp.float32)  36 us
    unnamed x172, local copies, waits for them, and re-layouts  32 us
    another operation x6, Pallas kernels  31.6 us
    psum x1, waiting for transfers between devices, device_fn(): lax.psum(dense_part, 'tp')  30.5 us
  transfers between devices with their start and end apart: 8, of which 4 were waited for; matrix products, arithmetic and copies ran while one was open for 36% of the time, Pallas kernels for 6%

commit v1 on v0

v1 whole, which is shorter than its diff:
```python
import functools
import math
import jax
import jax.numpy as jnp
from jax import lax
from jax.experimental import pallas as pl
from jax.experimental.pallas import tpu as pltpu
from jax.sharding import PartitionSpec as P

NORM_EPS = 1e-6
ROPE_THETA = 10000.0
MESH = pl.DeviceIdType.MESH
F32 = jnp.float32
BF16 = jnp.bfloat16
VMEM_ALL = 67043328


def rms_norm(values, gain):
    wide = values.astype(F32)
    mean_sq = jnp.mean(wide * wide, axis=-1, keepdims=True)
    return (wide * lax.rsqrt(mean_sq + NORM_EPS) * gain).astype(BF16)


def rope_tables(position, rope_dim):
    half_dim = rope_dim // 2
    inv_freq = ROPE_THETA ** (-(jnp.arange(half_dim, dtype=F32) * 2.0 / rope_dim))
    angles = position.astype(F32)[:, None] * inv_freq[None, :]
    return jnp.cos(angles), jnp.sin(angles)


def rotary(values, cos_t, sin_t):
    wide = values.astype(F32)
    half_dim = wide.shape[-1] // 2
    first = wide[..., :half_dim]
    second = wide[..., half_dim:]
    return jnp.concatenate([first * cos_t - second * sin_t, second * cos_t + first * sin_t], axis=-1)


def attention(normed, steps, pos, cos_t, sin_t, lat, rop, w_query, w_dkv, g_kv, w_uk, w_uv, w_out):
    rows = normed.shape[0]
    tokens = rows // steps
    heads, nope_dim = w_uk.shape[1], w_uk.shape[2]
    qk_dim = w_query.shape[2]
    lora = g_kv.shape[0]
    cache_len = lat.shape[1]
    query = jnp.einsum('bd,dhk->bhk', normed, w_query, preferred_element_type=F32)
    q_nope = query[..., :nope_dim].astype(BF16)
    q_rope = rotary(query[..., nope_dim:], cos_t[:, None, :], sin_t[:, None, :]).astype(BF16)
    kv_proj = jnp.dot(normed, w_dkv, preferred_element_type=F32)
    lat_new = rms_norm(kv_proj[:, :lora], g_kv).reshape(steps, tokens, -1)
    rope_new = rotary(kv_proj[:, lora:], cos_t, sin_t).astype(BF16).reshape(steps, tokens, -1)
    slot_ids = jnp.arange(cache_len)
    for s in range(steps):
        hit = (slot_ids[None, :] == (pos + s)[:, None])[:, :, None]
        lat = jnp.where(hit, lat_new[s][:, None, :], lat)
        rop = jnp.where(hit, rope_new[s][:, None, :], rop)
    q_lat = jnp.einsum('bhn,chn->bhc', q_nope, w_uk, preferred_element_type=F32).astype(BF16)

    def by_token(v):
        return v.reshape(steps, tokens, heads, -1).transpose(1, 0, 2, 3).reshape(tokens, steps * heads, -1)

    scores = (jnp.einsum('bhc,btc->bht', by_token(q_lat), lat, preferred_element_type=F32)
              + jnp.einsum('bhr,btr->bht', by_token(q_rope), rop, preferred_element_type=F32)) * (1.0 / math.sqrt(qk_dim))
    step_of = jnp.arange(steps * heads) // heads
    visible = slot_ids[None, None, :] <= pos[:, None, None] + step_of[None, :, None]
    scores = jnp.where(visible, scores, -1e30)
    prob = jax.nn.softmax(scores, axis=-1).astype(BF16)
    o_lat = jnp.einsum('bht,btc->bhc', prob, lat, preferred_element_type=F32).astype(BF16)
    o_lat = o_lat.reshape(tokens, steps, heads, -1).transpose(1, 0, 2, 3).reshape(rows, heads, -1)
    heads_out = jnp.einsum('bhc,chv->bhv', o_lat, w_uv, preferred_element_type=F32).astype(BF16)
    part = jnp.dot(heads_out.reshape(rows, -1), w_out, preferred_element_type=F32)
    return part, lat, rop


def swiglu(normed, w_gate, w_up, w_down):
    gate_h = jnp.dot(normed, w_gate, preferred_element_type=F32)
    up_h = jnp.dot(normed, w_up, preferred_element_type=F32)
    act = (jax.nn.silu(gate_h) * up_h).astype(BF16)
    return jnp.dot(act, w_down, preferred_element_type=F32)


def remote(src, dst, send, recv, where):
    return pltpu.make_async_remote_copy(src_ref=src, dst_ref=dst, send_sem=send, recv_sem=recv,
                                        device_id=where, device_id_type=MESH)


def turn(me, d, n):
    return lax.rem(me + d, n)


def reduce_kernel(n_tp, n_ep, with_ids, *refs):
    if with_ids:
        (part, resid, gain, ids, own_out, norm_out, ids_out,
         recv, gath, ids_all, s1, r1, s2, r2, s3, r3) = refs
    else:
        part, resid, gain, own_out, norm_out, recv, gath, s1, r1, s2, r2 = refs
    me = lax.axis_index("tp")
    rows = part.shape[0] // n_tp
    barrier = pltpu.get_barrier_semaphore()
    for d in range(1, n_tp):
        pl.semaphore_signal(barrier, inc=1, device_id={"tp": turn(me, d, n_tp)}, device_id_type=MESH)
    if with_ids:
        ep = lax.axis_index("ep")
        for d in range(1, n_ep):
            pl.semaphore_signal(barrier, inc=1, device_id={"ep": turn(ep, d, n_ep)}, device_id_type=MESH)
    pl.semaphore_wait(barrier, n_tp - 1 + (n_ep - 1 if with_ids else 0))
    sends = []
    for d in range(1, n_tp):
        peer = turn(me, d, n_tp)
        cp = remote(part.at[pl.ds(peer * rows, rows)], recv.at[d - 1], s1.at[d - 1], r1.at[d - 1], {"tp": peer})
        cp.start()
        sends.append(cp)
    id_sends = []
    if with_ids:
        for d in range(1, n_ep):
            cp = remote(ids, ids_all.at[ep], s3.at[d - 1], r3.at[d - 1], {"ep": turn(ep, d, n_ep)})
            cp.start()
            id_sends.append(cp)
        ids_out[ep] = ids[...]
    own_rows = pl.ds(me * rows, rows)
    base = resid[own_rows, :] if resid.shape[0] != rows else resid[...]
    total = part[own_rows, :]
    for d in range(1, n_tp):
        sends[d - 1].wait_recv()
        total = total + recv[d - 1]
    y = (base.astype(F32) + total).astype(BF16)
    own_out[...] = y
    normed = rms_norm(y, gain[...])
    gath[me] = normed
    gathers = []
    for d in range(1, n_tp):
        cp = remote(gath.at[me], gath.at[me], s2.at[d - 1], r2.at[d - 1], {"tp": turn(me, d, n_tp)})
        cp.start()
        gathers.append(cp)
    norm_out[own_rows, :] = normed
    for d in range(1, n_tp):
        gathers[d - 1].wait_recv()
        src = turn(me, n_tp - d, n_tp)
        norm_out[pl.ds(src * rows, rows), :] = gath[src]
    if with_ids:
        for d in range(1, n_ep):
            id_sends[d - 1].wait_recv()
            src = turn(ep, n_ep - d, n_ep)
            ids_out[src] = ids_all[src]
    for cp in sends + gathers + id_sends:
        cp.wait_send()


def reduce_norm(n_tp, n_ep, part, resid, gain, ids=None):
    rows, hidden = part.shape
    own = rows // n_tp
    out_shape = [jax.ShapeDtypeStruct((own, hidden), BF16), jax.ShapeDtypeStruct((rows, hidden), BF16)]
    scratch = [pltpu.VMEM((n_tp - 1, own, hidden), F32), pltpu.VMEM((n_tp, own, hidden), BF16)]
    sems = [pltpu.SemaphoreType.DMA((n_tp - 1,))] * 4
    args = [part, resid, gain[None, :]]
    if ids is not None:
        args.append(ids)
        out_shape.append(jax.ShapeDtypeStruct((n_ep,) + ids.shape, ids.dtype))
        scratch.append(pltpu.VMEM((n_ep,) + ids.shape, ids.dtype))
        sems += [pltpu.SemaphoreType.DMA((n_ep - 1,))] * 2
    vm = pl.BlockSpec(memory_space=pltpu.VMEM)
    return pl.pallas_call(
        functools.partial(reduce_kernel, n_tp, n_ep, ids is not None),
        out_shape=out_shape,
        in_specs=[vm] * len(args),
        out_specs=[vm] * len(out_shape),
        scratch_shapes=scratch + sems,
        compiler_params=pltpu.CompilerParams(collective_id=0 if ids is None else 1, has_side_effects=True),
        name="reduce_norm_ids" if ids is not None else "reduce_norm",
    )(*args)


def moe_kernel(n_tp, n_ep, part, resid, gain, router, ids, sg, su, sd, eg, eu, ed, out,
               wg, wu, wd, vg, vu, vd, xs, y_own, recv, comb, acc, drecv, xrecv, shbuf, yrecv, obuf,
               wsem, vsem, s1, r1, sx, rx, sy, ry, sd2, rd2, sa, ra, sb, rb, sc, rc, so, ro):
    me = lax.axis_index("tp")
    ep = lax.axis_index("ep")
    xi, core = ep // 2, lax.rem(ep, 2)
    n_x = n_ep // 2
    partner = ep + 1 - 2 * core
    rows = part.shape[0] // n_tp
    hidden = part.shape[1]
    block = part.shape[0]
    n_exp = wg.shape[0]

    loads = []
    for i, (src, dst) in enumerate(((sg, vg), (su, vu), (sd, vd))):
        cp = pltpu.make_async_copy(src, dst, vsem.at[i])
        cp.start()
        loads.append(cp)
    for e in range(n_exp):
        for i, (src, dst) in enumerate(((eg, wg), (eu, wu), (ed, wd))):
            pltpu.make_async_copy(src.at[e], dst.at[e], wsem.at[i, e]).start()

    barrier = pltpu.get_barrier_semaphore()
    for d in range(1, n_tp):
        pl.semaphore_signal(barrier, inc=1, device_id={"tp": turn(me, d, n_tp)}, device_id_type=MESH)
    for d in range(1, n_x):
        pl.semaphore_signal(barrier, inc=1, device_id={"ep": turn(ep, 2 * d, n_ep)}, device_id_type=MESH)
    pl.semaphore_signal(barrier, inc=1, device_id={"ep": partner}, device_id_type=MESH)
    pl.semaphore_wait(barrier, n_tp - 1 + n_x - 1 + 1)

    pend = []
    cps = []
    for d in range(1, n_tp):
        peer = turn(me, d, n_tp)
        cp = remote(part.at[pl.ds(peer * rows, rows)], recv.at[d - 1], s1.at[d - 1], r1.at[d - 1], {"tp": peer})
        cp.start()
        cps.append(cp)
    total = part[pl.ds(me * rows, rows), :]
    for d in range(1, n_tp):
        cps[d - 1].wait_recv()
        total = total + recv[d - 1]
    pend += cps
    y = (resid[...].astype(F32) + total).astype(BF16)
    y_own[...] = y
    xs[ep, me] = rms_norm(y, gain[...])

    xcp, ycp = [], {}
    for d in range(1, n_x):
        cp = remote(xs.at[ep, me], xs.at[ep, me], sx.at[d - 1], rx.at[d - 1], {"ep": turn(ep, 2 * d, n_ep)})
        cp.start()
        xcp.append(cp)
    for k in range(n_x):
        src_ep = turn(ep, n_ep - 2 * k, n_ep)
        if k:
            xcp[k - 1].wait_recv()
        for d in range(1, n_tp):
            cp = remote(xs.at[src_ep, me], xs.at[src_ep, me], sy.at[k, d - 1], ry.at[k, d - 1], {"tp": turn(me, d, n_tp)})
            cp.start()
            ycp[k, d] = cp
    pcp = []
    for k in range(n_x):
        src_ep = turn(ep, n_ep - 2 * k, n_ep)
        for d in range(1, n_tp):
            ycp[k, d].wait_recv()
        cp = remote(xs.at[src_ep], xs.at[src_ep], sd2.at[k], rd2.at[k], {"ep": partner})
        cp.start()
        pcp.append(cp)
    pend += xcp + list(ycp.values()) + pcp

    for cp in loads:
        cp.wait()
    own = xs[ep].reshape(block, hidden)
    sact = (jax.nn.silu(jnp.dot(own, vg[...], preferred_element_type=F32))
            * jnp.dot(own, vu[...], preferred_element_type=F32)).astype(BF16)
    shbuf[...] = jnp.dot(sact, vd[...], preferred_element_type=F32)
    for cp in pcp:
        cp.wait_recv()

    for k in range(n_x):
        xk = xs[2 * k:2 * k + 2].reshape(2 * block, hidden)
        logits = jnp.dot(xk, router[...], preferred_element_type=F32)
        top = jnp.max(logits, axis=-1, keepdims=True)
        ex = jnp.exp(logits - top)
        prob = ex / jnp.sum(ex, axis=-1, keepdims=True)
        lane = lax.broadcasted_iota(jnp.int32, prob.shape, 1)
        picks = ids[2 * k:2 * k + 2].reshape(2 * block, ids.shape[-1])
        chosen = lane == picks[:, 0:1]
        for j in range(1, TOP_K[0]):
            chosen = chosen | (lane == picks[:, j:j + 1])
        comb[k] = jnp.where(chosen, prob, 0.0)

    n_col = 4
    width = hidden // n_col

    def experts(slot, xb, first, lo, hi):
        def body(e, _):
            if first:
                for i, (src, dst) in enumerate(((eg, wg), (eu, wu), (ed, wd))):
                    pltpu.make_async_copy(src.at[e], dst.at[e], wsem.at[i, e]).wait()
            xk = xs[pl.ds(2 * xb, 2)].reshape(2 * block, hidden)
            gate = jnp.dot(xk, wg[e], preferred_element_type=F32)
            up = jnp.dot(xk, wu[e], preferred_element_type=F32)
            act = (jax.nn.silu(gate) * up).astype(BF16)
            cw = comb[xb]
            lane = lax.broadcasted_iota(jnp.int32, cw.shape, 1)
            col = jnp.sum(jnp.where(lane == ep * n_exp + e, cw, 0.0), axis=-1, keepdims=True)
            for q in range(n_col):
                cs = slice(q * width, (q + 1) * width)
                acc[slot, :, cs] += col * jnp.dot(act, wd[e, :, cs], preferred_element_type=F32)
            return 0
        lax.fori_loop(lo, hi, body, 0)

    order = [2, 1, 3, 0] if n_x == 4 else list(range(1, n_x)) + [0]
    dcp, acp = {}, {}
    mine = pl.ds(core * block, block)
    other = pl.ds((1 - core) * block, block)

    def settle(b):
        dcp[b].wait_recv()
        drecv[b] = drecv[b] + acc[b % 2, mine, :]
        d = order[b]
        if d:
            cp = remote(drecv.at[b], xrecv.at[d - 1], sa.at[d - 1], ra.at[d - 1], {"ep": turn(ep, 2 * d, n_ep)})
            cp.start()
            acp[d] = cp
        dcp[b].wait_send()

    half = n_exp // 2
    for b, d in enumerate(order):
        slot = b % 2
        xb = lax.rem(xi + d, n_x)
        acc[slot] = jnp.zeros(acc.shape[1:], F32)
        experts(slot, xb, b == 0, 0, half)
        if b:
            settle(b - 1)
        experts(slot, xb, b == 0, half, n_exp)
        cp = remote(acc.at[slot, other], drecv.at[b], sb.at[b], rb.at[b], {"ep": partner})
        cp.start()
        dcp[b] = cp
    last = n_x - 1
    settle(last)
    drecv[last] = drecv[last] + shbuf[...]
    for d in range(1, n_x):
        acp[d].wait_recv()
        drecv[last] = drecv[last] + xrecv[d - 1]
    pend += list(acp.values())
    ccp = []
    for d in range(1, n_tp):
        peer = turn(me, d, n_tp)
        cp = remote(drecv.at[last, pl.ds(peer * rows, rows)], yrecv.at[d - 1], sc.at[d - 1], rc.at[d - 1], {"tp": peer})
        cp.start()
        ccp.append(cp)
    total = drecv[last, pl.ds(me * rows, rows), :]
    for d in range(1, n_tp):
        ccp[d - 1].wait_recv()
        total = total + yrecv[d - 1]
    fin = (y_own[...].astype(F32) + total).astype(BF16)
    obuf[me] = fin
    ocp = []
    for d in range(1, n_tp):
        cp = remote(obuf.at[me], obuf.at[me], so.at[d - 1], ro.at[d - 1], {"tp": turn(me, d, n_tp)})
        cp.start()
        ocp.append(cp)
    out[pl.ds(me * rows, rows), :] = fin
    for d in range(1, n_tp):
        ocp[d - 1].wait_recv()
        src = turn(me, n_tp - d, n_tp)
        out[pl.ds(src * rows, rows), :] = obuf[src]
    for cp in pend + ccp + ocp:
        cp.wait_send()


TOP_K = [6]


def moe(n_tp, n_ep, part, resid, gain, router, ids, sg, su, sd, eg, eu, ed):
    rows, hidden = part.shape
    own = rows // n_tp
    n_x = n_ep // 2
    dma = pltpu.SemaphoreType.DMA
    n_exp = eg.shape[0]
    vm = pl.BlockSpec(memory_space=pltpu.VMEM)
    hbm = pl.BlockSpec(memory_space=pl.ANY)
    scratch = [
        pltpu.VMEM(eg.shape, BF16), pltpu.VMEM(eu.shape, BF16), pltpu.VMEM(ed.shape, BF16),
        pltpu.VMEM(sg.shape, BF16), pltpu.VMEM(su.shape, BF16), pltpu.VMEM(sd.shape, BF16),
        pltpu.VMEM((n_ep, n_tp, own, hidden), BF16),
        pltpu.VMEM((own, hidden), BF16),
        pltpu.VMEM((n_tp - 1, own, hidden), F32),
        pltpu.VMEM((n_x, 2 * rows, router.shape[1]), F32),
        pltpu.VMEM((2, 2 * rows, hidden), F32),
        pltpu.VMEM((n_x, rows, hidden), F32),
        pltpu.VMEM((n_x - 1, rows, hidden), F32),
        pltpu.VMEM((rows, hidden), F32),
        pltpu.VMEM((n_tp - 1, own, hidden), F32),
        pltpu.VMEM((n_tp, own, hidden), BF16),
        dma((3, n_exp)), dma((3,)),
        dma((n_tp - 1,)), dma((n_tp - 1,)),
        dma((n_x - 1,)), dma((n_x - 1,)),
        dma((n_x, n_tp - 1)), dma((n_x, n_tp - 1)),
        dma((n_x,)), dma((n_x,)),
        dma((n_x - 1,)), dma((n_x - 1,)),
        dma((n_x,)), dma((n_x,)),
        dma((n_tp - 1,)), dma((n_tp - 1,)),
        dma((n_tp - 1,)), dma((n_tp - 1,)),
    ]
    return pl.pallas_call(
        functools.partial(moe_kernel, n_tp, n_ep),
        out_shape=jax.ShapeDtypeStruct((rows, hidden), BF16),
        in_specs=[vm] * 5 + [hbm] * 6,
        out_specs=vm,
        scratch_shapes=scratch,
        compiler_params=pltpu.CompilerParams(collective_id=2, has_side_effects=True, vmem_limit_bytes=VMEM_ALL),
        name="moe",
    )(part, resid, gain[None, :], router, ids, sg, su, sd, eg, eu, ed)


def solution(mesh):
    tok_axes = ('dp', 'ep')
    n_tp, n_ep = mesh.shape['tp'], mesh.shape['ep']

    def device_fn(emb, pos, route_ids, lat_cache, rope_cache, attn_norm, w_q, w_dkv, kv_norm, w_uk, w_uv, w_o, mlp_norm, dense_gate, dense_up, dense_down, router, shared_gate, shared_up, shared_down, expert_gate, expert_up, expert_down):
        steps, tokens, hidden = emb.shape
        rows = steps * tokens
        TOP_K[0] = route_ids.shape[-1]
        emb_rows = emb.reshape(rows, hidden)
        ids = jnp.pad(route_ids.reshape(rows, -1), ((0, 0), (0, 128 - route_ids.shape[-1])), constant_values=-1)
        all_pos = jnp.concatenate([pos + s for s in range(steps)])
        cos_t, sin_t = rope_tables(all_pos, rope_cache.shape[-1])

        def attend(layer, normed):
            return attention(normed, steps, pos, cos_t, sin_t, lat_cache[layer], rope_cache[layer], w_q[layer], w_dkv[layer], kv_norm[layer], w_uk[layer], w_uv[layer], w_o[layer])

        part, lat0, rop0 = attend(0, rms_norm(emb_rows, attn_norm[0]))
        y_own, normed, ids_all = reduce_norm(n_tp, n_ep, part, emb_rows, mlp_norm[0], ids)
        part = swiglu(normed, dense_gate, dense_up, dense_down)
        h_own, normed = reduce_norm(n_tp, n_ep, part, y_own, attn_norm[1])
        part, lat1, rop1 = attend(1, normed)
        out = moe(n_tp, n_ep, part, h_own, mlp_norm[1], router, ids_all, shared_gate, shared_up, shared_down, expert_gate, expert_up, expert_down)
        return out.reshape(steps, tokens, hidden), jnp.stack([lat0, lat1]), jnp.stack([rop0, rop1])

    in_specs = (P(None, tok_axes, None), P(tok_axes), P(None, tok_axes, None), P(None, tok_axes, None, None), P(None, tok_axes, None, None), P(), P(None, None, 'tp', None), P(), P(), P(None, None, 'tp', None), P(None, None, 'tp', None), P(None, 'tp', None), P(), P(None, 'tp'), P(None, 'tp'), P('tp', None), P(), P(None, 'tp'), P(None, 'tp'), P('tp', None), P('ep', None, 'tp'), P('ep', None, 'tp'), P('ep', 'tp', None))
    out_specs = (P(None, tok_axes, None), P(None, tok_axes, None, None), P(None, tok_axes, None, None))
    return jax.shard_map(device_fn, mesh=mesh, in_specs=in_specs, out_specs=out_specs, check_vma=False)
```

time: 635 us -> 252 us (0.40); the launches traced: 625 us -> 251 us
  waiting for transfers between devices: 120 us -> 0 us
  other arithmetic: 121 us -> 20.3 us
  blocking collectives: 97.8 us -> 0 us
  Pallas kernels: 34.6 us -> 122 us
  local copies, waits for them, and re-layouts: 114 us -> 47.8 us
  matrix products: 120 us -> 59.8 us
  between operations: 15.8 us -> 1.17 us
    pallas_call x0 -> x3, Pallas kernels: none -> 122 us  [the longest x1 84.7 us: moe(): pl.pallas_call(functools.partial(moe_kernel, n_tp, n_ep), out_shape=jax.S...]
    all_gather x4 -> x0, blocking collectives: 97.8 us -> none  [the longest x2 52.7 us: routed_local(): weight_all = lax.all_gather(route_w, 'ep', axis=0, tiled=True)]
    psum x4 -> x0, waiting for transfers between devices: 95.5 us -> none  [the longest x2 37.9 us: device_fn(): lax.psum(attn_part, 'tp')]
    gather x16 -> x0, local copies, waits for them, and re-layouts: 71.1 us -> none  [the longest x2 28.1 us: routed_local(): sorted_rows = jnp.take(tok_all, tok_index, axis=0)]
    dot_general x38 -> x16, matrix products: 111 us -> 55.9 us  [the longest x1 13.7 us: swiglu(): return jnp.dot(act, w_down, preferred_element_type=F32)]
    scatter-add x2 -> x0, other arithmetic: 47.3 us -> none  [routed_local(): jax.ops.segment_sum(contrib, tok_index, num_segments=tok_all.shape[0])]
    another operation x6 -> x0, Pallas kernels: 31.6 us -> none
    reduce_scatter x2 -> x0, waiting for transfers between devices: 24.4 us -> none  [routed_local(): return lax.psum_scatter(token_sum, 'ep', scatter_dimension=0, tiled=True)]
  transfers between devices with their start and end apart: 8 -> 0, of which waited for: 4 -> 0; matrix products, arithmetic and copies ran while one was open for 36% -> 0% of each run, Pallas kernels for 6% -> 0%
where the time goes in v1:
time: 252 us; the launch traced here: 251 us
  Pallas kernels  122 us (48%)
  matrix products  59.8 us (24%)
  local copies, waits for them, and re-layouts  47.8 us (19%)
  other arithmetic  20.3 us (8%)
    pallas_call x1, Pallas kernels, moe(): pl.pallas_call(functools.partial(moe_kernel, n_tp, n_ep), out_shape=jax.S...  84.7 us
    unnamed x61, local copies, waits for them, and re-layouts  40.9 us
    pallas_call x2, Pallas kernels, reduce_norm(): pl.pallas_call(functools.partial(reduce_kernel, n_tp, n_ep, ids is not No...  37 us
    dot_general x1, matrix products, swiglu(): return jnp.dot(act, w_down, preferred_element_type=F32)  13.7 us
    dot_general x2, matrix products, attention(): jnp.einsum('bhc,btc->bht', by_token(q_lat), lat, preferred_element_type=F32)  8.54 us
    dot_general x1, matrix products, swiglu(): gate_h = jnp.dot(normed, w_gate, preferred_element_type=F32)  7.79 us
    dot_general x2, matrix products, attention(): jnp.einsum('bht,btc->bhc', prob, lat, preferred_element_type=F32)  6.97 us
    another operation x1, other arithmetic, device_fn(): jnp.stack([lat0, lat1])  6.43 us

profile of v1, /device:TPU:96, one launch (start us, length us, event | category | flops | bytes accessed | tf_op | source)
XLA Modules:
  0.0 250.8 jit_solution(13511774699501064294)
XLA Ops:
  0.6 0.7 broadcast_add_fusion.1
  1.4 0.7 iota_compare_fusion.1
  2.1 1.4 fusion.105
  3.5 1.1 fusion.56
  4.6 1.1 fusion.58
  5.7 2.5 fusion.21
  8.2 0.8 fusion.106
  9.0 0.1 multiply_reduce_fusion.1
  9.1 0.1 multiply_convert_fusion.1
  9.3 0.4 fusion.101
  9.6 3.0 %fusion.7 = f32[64,4,192]{2,0,1:T(8,128)S(1)} fusion(bf16[64,2048,1]{1,0,2:T(8,128)(2,1)S(1)} %bitcast.133, bf16[2,2048,4,192]{1,3,2,0:T(8,128)(2,1)} %param.29), kind=kOutput, calls=%fused_computation.13 | convolution fusion | flops 201326592 | bytes 3604480 | tf_op jit(solution)/shard_map/bd,dhk->bhk/dot_general | solution.py:46
  12.6 0.3 convolution_convert_fusion.1
  12.9 0.2 copy.43
  13.2 0.1 reshape.299
  13.2 4.3 %fusion.13 = f32[32,8,128]{2,1,0:T(8,128)S(1)} fusion(bf16[32,8,512]{2,1,0:T(8,128)(2,1)S(1)} %reshape.299, pred[32,128]{1,0:T(8,128)(4,1)S(1)} %get-tuple-element.49, pred[32,128]{1,0:T(8,128)(4,1)S(1)} %get-tuple-element.50, bf16[2,32,128,512]{3,2,1,0:T(8,128)(2,1)} %param.26, bf16[32,512]{1,0:T(8,128)(2,1)S(1)} %get-tuple-element.32, ...), kind=kOutput, calls=%fused_computation.18 | convolution fusion | flops 37748736 | bytes 4661248 | tf_op jit(solution)/shard_map/bhc,btc->bht/dot_general | solution.py:62
  17.6 0.1 add_convert_fusion.2
  17.7 0.2 fusion.90
  17.9 0.1 subtract_convert_fusion.1
  18.0 0.1 maximum_bitcast_fusion
  18.1 0.1 fusion.98
  18.2 0.1 broadcast_add_fusion
  18.3 1.9 fusion.107
  20.3 3.2 %fusion.42 = bf16[32,8,512]{2,1,0:T(8,128)(2,1)S(1)} fusion(pred[32,128]{1,0:T(8,128)(4,1)S(1)} %get-tuple-element.49, pred[32,128]{1,0:T(8,128)(4,1)S(1)} %get-tuple-element.50, bf16[2,32,128,512]{3,2,1,0:T(8,128)(2,1)} %param.26, bf16[32,512]{1,0:T(8,128)(2,1)S(1)} %get-tuple-element.32, bf16[32,512]{1,0:T(8,128)(2,1)S(1)} %get-tuple-element.31, ...), kind=kOutput, calls=%fused_computation.42 | convolution fusion | flops 37945344 | bytes 4662272 | tf_op jit(solution)/shard_map/bht,btc->bhc/dot_general | solution.py:68
  23.5 0.1 reshape.301
  23.5 0.1 copy.45
  23.6 1.2 fusion.100
  24.8 0.2 fusion.53
  25.0 2.9 %fusion.27.refs_0_ = f32[64,2048]{1,0:T(8,128)} fusion(bf16[2,512,2048]{2,1,0:T(8,128)(2,1)} %param.34, bf16[4,8,8,128]{3,2,1,0:T(8,128)(2,1)S(1)} %fusion.53), kind=kOutput, calls=%fused_computation.29 | convolution fusion | flops 134217728 | bytes 2686976 | tf_op jit(solution)/shard_map/dot_general | solution.py:71
  27.9 0.6 fusion.104
  28.5 0.1 copy.48
  28.6 0.6 pad.4.refs_3_
  29.2 21.1 %reduce_norm_ids.1 = (bf16[16,2048]{1,0:T(8,128)(2,1)}, bf16[64,2048]{1,0:T(8,128)(2,1)}, s32[8,64,128]{2,1,0:T(8,128)}) custom-call(f32[64,2048]{1,0:T(8,128)} %fusion.27.refs_0_, bf16[64,2048]{1,0:T(8,128)(2,1)} %bitcast.122, f32[1,2048]{1,0:T(1,128)} %get-tuple-element.38.refs_2_, s32[64,128]{1,0:T(8,128)} %pad.4.refs_3_), custom_call_target="tpu_custom_call" | custom-call | tf_op jit(solution)/shard_map/reduce_norm_ids/pallas_call | solution.py:162
  50.4 7.8 %fusion.113 = f32[64,2736]{1,0:T(8,128)S(1)} fusion(bf16[64,2048]{1,0:T(8,128)(2,1)} %get-tuple-element.8, bf16[2048,2736]{0,1:T(8,128)(2,1)} %param.36), kind=kOutput, calls=%fused_computation.158 | convolution fusion | flops 717225984 | bytes 12169216 | tf_op jit(solution)/shard_map/dot_general | solution.py:76
  58.2 13.7 %fusion.55.refs_0_ = f32[64,2048]{1,0:T(8,128)} fusion(bf16[2736,2048]{1,0:T(8,128)(2,1)} %param.38, bf16[64,2048]{1,0:T(8,128)(2,1)S(1)} %copy-done.1, bf16[2048,2736]{0,1:T(8,128)(2,1)} %param.37, f32[64,2736]{1,0:T(8,128)S(1)} %fusion.113), kind=kOutput, calls=%fused_computation.62 | convolution fusion | flops 1435502592 | bytes 23900160 | tf_op jit(solution)/shard_map/dot_general | solution.py:79
  71.8 15.9 %reduce_norm.1 = (bf16[16,2048]{1,0:T(8,128)(2,1)}, bf16[64,2048]{1,0:T(8,128)(2,1)}) custom-call(f32[64,2048]{1,0:T(8,128)} %fusion.55.refs_0_, bf16[16,2048]{1,0:T(8,128)(2,1)} %get-tuple-element.9.refs_1_, f32[1,2048]{1,0:T(1,128)} %get-tuple-element.39.refs_2_), custom_call_target="tpu_custom_call" | custom-call | tf_op jit(solution)/shard_map/reduce_norm/pallas_call | solution.py:162
  87.7 2.6 %fusion.19 = f32[64,576]{1,0:T(8,128)S(1)} fusion(bf16[64,2048]{1,0:T(8,128)(2,1)} %get-tuple-element.10, bf16[2,2048,576]{1,2,0:T(8,128)(2,1)} %param.30), kind=kOutput, calls=%fused_computation.21 | convolution fusion | flops 150994944 | bytes 2768896 | tf_op jit(solution)/shard_map/dot_general | solution.py:49
  90.3 0.1 multiply_reduce_fusion
  90.4 0.1 multiply_convert_fusion
  90.6 3.1 %fusion.5 = f32[64,4,192]{2,0,1:T(8,128)S(1)} fusion(bf16[2,2048,4,192]{1,3,2,0:T(8,128)(2,1)} %param.29, bf16[64,2048]{1,0:T(8,128)(2,1)} %get-tuple-element.10), kind=kOutput, calls=%fused_computation.11 | convolution fusion | flops 201326592 | bytes 3604480 | tf_op jit(solution)/shard_map/bd,dhk->bhk/dot_general | solution.py:46
  93.7 0.3 convolution_convert_fusion
  94.0 0.2 copy.50
  94.2 0.1 reshape.307
  94.3 4.2 %fusion.17 = f32[32,8,128]{2,1,0:T(8,128)S(1)} fusion(bf16[32,8,512]{2,1,0:T(8,128)(2,1)S(1)} %reshape.307, pred[32,128]{1,0:T(8,128)(4,1)S(1)} %get-tuple-element.49, pred[32,128]{1,0:T(8,128)(4,1)S(1)} %get-tuple-element.50, bf16[2,32,128,512]{3,2,1,0:T(8,128)(2,1)} %param.26, bf16[32,512]{1,0:T(8,128)(2,1)S(1)} %get-tuple-element.30, ...), kind=kOutput, calls=%fused_computation.20 | convolution fusion | flops 37748736 | bytes 4661248 | tf_op jit(solution)/shard_map/bhc,btc->bht/dot_general | solution.py:62
  98.5 0.1 subtract_convert_fusion
  98.7 0.1 maximum_bitcast_fusion.1
  98.8 0.2 fusion.94
  99.0 0.1 fusion.97
  99.1 1.9 fusion.108
  101.1 3.8 %fusion.39 = bf16[32,8,512]{2,1,0:T(8,128)(2,1)} fusion(pred[32,128]{1,0:T(8,128)(4,1)S(1)} %get-tuple-element.49, pred[32,128]{1,0:T(8,128)(4,1)S(1)} %get-tuple-element.50, bf16[2,32,128,512]{3,2,1,0:T(8,128)(2,1)} %param.26, bf16[32,512]{1,0:T(8,128)(2,1)S(1)} %get-tuple-element.30, bf16[32,512]{1,0:T(8,128)(2,1)S(1)} %get-tuple-element.29, ...), kind=kOutput, calls=%fused_computation.41 | convolution fusion | flops 37945344 | bytes 4662272 | tf_op jit(solution)/shard_map/bht,btc->bhc/dot_general | solution.py:68
  104.9 1.2 reshape.309
  106.0 0.1 copy.52
  106.1 1.3 fusion.54
  107.4 2.9 %fusion.25.part = f32[64,2048]{1,0:T(8,128)} fusion(bf16[2,512,2048]{2,1,0:T(8,128)(2,1)} %param.34, bf16[4,8,8,128]{3,2,1,0:T(8,128)(2,1)S(1)} %fusion.54), kind=kOutput, calls=%fused_computation.27 | convolution fusion | flops 134217728 | bytes 2686976 | tf_op jit(solution)/shard_map/dot_general | solution.py:71
  110.3 1.0 copy.55.router
  111.3 2.8 %copy.56.sg = bf16[2048,704]{1,0:T(8,128)(2,1)} copy(bf16[2048,704]{0,1:T(8,128)(2,1)S(1)} %copy-done) | data formatting | bytes 5767168 | tf_op args[17]
  114.0 4.7 %copy.57.su = bf16[2048,704]{1,0:T(8,128)(2,1)} copy(bf16[2048,704]{0,1:T(8,128)(2,1)} %param.41) | data formatting | bytes 5767168 | tf_op args[18]
  118.7 16.2 %copy.58.eg = bf16[8,2048,352]{2,1,0:T(8,128)(2,1)} copy(bf16[8,2048,352]{1,2,0:T(8,128)(2,1)} %param.43) | data formatting | bytes 23068672 | tf_op args[20]
  134.9 15.3 %copy.59.eu = bf16[8,2048,352]{2,1,0:T(8,128)(2,1)} copy(bf16[8,2048,352]{1,2,0:T(8,128)(2,1)} %param.44) | data formatting | bytes 23068672 | tf_op args[21]
  150.2 84.7 %moe.1 = bf16[64,2048]{1,0:T(8,128)(2,1)} custom-call(f32[64,2048]{1,0:T(8,128)} %fusion.25.part, bf16[16,2048]{1,0:T(8,128)(2,1)} %get-tuple-element.11.resid, f32[1,2048]{1,0:T(1,128)} %get-tuple-element.37.gain, bf16[2048,64]{1,0:T(8,128)(2,1)} %copy.55.router, s32[8,64,128]{2,1,0:T(8,128)} %get-tuple-element.12.ids, bf16[2048,704]{1,0:T(8,128)(2,1)} %copy.56.sg, ...), custom_call_target="tpu_custom_call" | custom-call | tf_op jit(solution)/shard_map/moe/pallas_call | solution.py:379
  234.9 6.4 %select_select_fusion.1 = (bf16[1,32,128,512]{3,2,1,0:T(8,128)(2,1)S(1)}, bf16[1,32,128,512]{3,2,1,0:T(8,128)(2,1)}) fusion(pred[32,128]{1,0:T(8,128)(4,1)} %copy-done.12, pred[32,128]{1,0:T(8,128)(4,1)} %copy-done.14, bf16[2,32,128,512]{3,2,1,0:T(8,128)(2,1)} %param.26, bf16[32,512]{1,0:T(8,128)(2,1)} %copy-done.9, bf16[32,512]{1,0:T(8,128)(2,1)} %copy-done.8, ...), kind=kLoop, calls=%fused_computation.8 | loop fusion | flops 8388608 | bytes 16916480 | tf_op jit(solution)/shard_map/jit(_where)/select_n | solution.py:55
  241.3 6.4 %pad_maximum_fusion = bf16[2,32,128,512]{3,2,1,0:T(8,128)(2,1)} fusion(bf16[1,32,128,512]{3,2,1,0:T(8,128)(2,1)} %get-tuple-element.14, bf16[1,32,128,512]{3,2,1,0:T(8,128)(2,1)S(1)} %get-tuple-element.13), kind=kLoop, calls=%fused_computation.2 | loop fusion | flops 4194304 | bytes 16777216 | tf_op jit(solution)/shard_map/stack | solution.py:412
  247.8 1.3 select_select_fusion.3
  249.1 1.1 pad_maximum_fusion.1
  250.1 0.7 copy.83
  (63 shorter events, 0.3 us)
Async XLA Ops:
  0.6 8.6 %copy-start.3 = (bf16[2,512,4,128]{3,2,1,0:T(4,128)(2,1)S(1)}, bf16[2,512,4,128]{3,2,1,0:T(4,128)(2,1)}, u32[]{:S(2)}) copy-start(bf16[2,512,4,128]{3,2,1,0:T(4,128)(2,1)} %param.32) | copy-start | bytes 3145732
  2.1 98.9 %copy-start.12 = (pred[32,128]{1,0:T(8,128)(4,1)}, pred[32,128]{1,0:T(8,128)(4,1)S(1)}, u32[]{:S(2)}) copy-start(pred[32,128]{1,0:T(8,128)(4,1)S(1)} %get-tuple-element.49) | copy-start | bytes 12292
  2.1 98.9 %copy-start.14 = (pred[32,128]{1,0:T(8,128)(4,1)}, pred[32,128]{1,0:T(8,128)(4,1)S(1)}, u32[]{:S(2)}) copy-start(pred[32,128]{1,0:T(8,128)(4,1)S(1)} %get-tuple-element.50) | copy-start | bytes 12292
  9.2 11.0 %copy-start.8 = (bf16[32,512]{1,0:T(8,128)(2,1)}, bf16[32,512]{1,0:T(8,128)(2,1)S(1)}, u32[]{:S(2)}) copy-start(bf16[32,512]{1,0:T(8,128)(2,1)S(1)} %get-tuple-element.31) | copy-start | bytes 98308
  9.2 11.0 %copy-start.9 = (bf16[32,512]{1,0:T(8,128)(2,1)}, bf16[32,512]{1,0:T(8,128)(2,1)S(1)}, u32[]{:S(2)}) copy-start(bf16[32,512]{1,0:T(8,128)(2,1)S(1)} %get-tuple-element.32) | copy-start | bytes 98308
  13.2 4.4 %copy-start.26 = (s32[32]{0:T(128)S(1)}, s32[32]{0:T(128)}, u32[]{:S(2)}) copy-start(s32[32]{0:T(128)} %param.24) | copy-start | bytes 388
  13.2 5.1 %copy-start.5 = (bf16[2,32,128,64]{2,3,1,0:T(8,128)(2,1)S(1)}, bf16[2,32,128,64]{2,3,1,0:T(8,128)(2,1)}, u32[]{:S(2)}) copy-start(bf16[2,32,128,64]{2,3,1,0:T(8,128)(2,1)} %param.27) | copy-start | bytes 3145732
  18.2 2.0 copy-start.16
  18.2 2.0 copy-start.18
  20.3 3.4 %copy-start.4 = (bf16[2,512,4,128]{3,2,1,0:T(4,128)(2,1)S(1)}, bf16[2,512,4,128]{3,2,1,0:T(4,128)(2,1)}, u32[]{:S(2)}) copy-start(bf16[2,512,4,128]{3,2,1,0:T(4,128)(2,1)} %param.33) | copy-start | bytes 3145732
  23.5 4.4 %copy-start.24 = (f32[2,2048]{1,0:T(2,128)S(1)}, f32[2,2048]{1,0:T(2,128)}, u32[]{:S(2)}) copy-start(f32[2,2048]{1,0:T(2,128)} %param.35) | copy-start | bytes 49156
  23.5 5.0 %copy-start.25 = (s32[2,32,6]{1,0,2:T(2,128)S(1)}, s32[2,32,6]{1,0,2:T(2,128)}, u32[]{:S(2)}) copy-start(s32[2,32,6]{1,0,2:T(2,128)} %param.25) | copy-start | bytes 4612
  50.4 7.8 %copy-start.1 = (bf16[64,2048]{1,0:T(8,128)(2,1)S(1)}, bf16[64,2048]{1,0:T(8,128)(2,1)}, u32[]{:S(2)}) copy-start(bf16[64,2048]{1,0:T(8,128)(2,1)} %get-tuple-element.8) | copy-start | bytes 786436
  90.6 10.5 %copy-start.10 = (bf16[32,512]{1,0:T(8,128)(2,1)}, bf16[32,512]{1,0:T(8,128)(2,1)S(1)}, u32[]{:S(2)}) copy-start(bf16[32,512]{1,0:T(8,128)(2,1)S(1)} %get-tuple-element.29) | copy-start | bytes 98308
  90.6 10.5 %copy-start.11 = (bf16[32,512]{1,0:T(8,128)(2,1)}, bf16[32,512]{1,0:T(8,128)(2,1)S(1)}, u32[]{:S(2)}) copy-start(bf16[32,512]{1,0:T(8,128)(2,1)S(1)} %get-tuple-element.30) | copy-start | bytes 98308
  99.1 2.0 copy-start.20
  99.1 2.0 copy-start.22
  104.9 5.4 %copy-start.7 = (bf16[2048,64]{0,1:T(8,128)(2,1)S(1)}, bf16[2048,64]{0,1:T(8,128)(2,1)}, u32[]{:S(2)}) copy-start(bf16[2048,64]{0,1:T(8,128)(2,1)} %param.39) | copy-start | bytes 786436
  104.9 6.4 %copy-start = (bf16[2048,704]{0,1:T(8,128)(2,1)S(1)}, bf16[2048,704]{0,1:T(8,128)(2,1)}, u32[]{:S(2)}) copy-start(bf16[2048,704]{0,1:T(8,128)(2,1)} %param.40) | copy-start | bytes 8650756
  241.2 6.5 %copy-start.6 = (bf16[2,32,128,64]{2,3,1,0:T(8,128)(2,1)S(1)}, bf16[2,32,128,64]{2,3,1,0:T(8,128)(2,1)}, u32[]{:S(2)}) copy-start(bf16[2,32,128,64]{2,3,1,0:T(8,128)(2,1)} %param.27) | copy-start | bytes 3145732
  241.2 6.5 %copy-start.13 = (pred[32,128]{1,0:T(8,128)(4,1)S(1)}, pred[32,128]{1,0:T(8,128)(4,1)}, u32[]{:S(2)}) copy-start(pred[32,128]{1,0:T(8,128)(4,1)} %copy-done.12) | copy-start | bytes 12292
  241.3 6.5 %copy-start.15 = (pred[32,128]{1,0:T(8,128)(4,1)S(1)}, pred[32,128]{1,0:T(8,128)(4,1)}, u32[]{:S(2)}) copy-start(pred[32,128]{1,0:T(8,128)(4,1)} %copy-done.14) | copy-start | bytes 12292
  241.3 6.5 %copy-start.17 = (bf16[32,64]{1,0:T(8,128)(2,1)S(1)}, bf16[32,64]{1,0:T(8,128)(2,1)}, u32[]{:S(2)}) copy-start(bf16[32,64]{1,0:T(8,128)(2,1)} %copy-done.16) | copy-start | bytes 12292
  241.3 6.5 %copy-start.19 = (bf16[32,64]{1,0:T(8,128)(2,1)S(1)}, bf16[32,64]{1,0:T(8,128)(2,1)}, u32[]{:S(2)}) copy-start(bf16[32,64]{1,0:T(8,128)(2,1)} %copy-done.18) | copy-start | bytes 12292
  241.3 6.5 %copy-start.21 = (bf16[32,64]{1,0:T(8,128)(2,1)S(1)}, bf16[32,64]{1,0:T(8,128)(2,1)}, u32[]{:S(2)}) copy-start(bf16[32,64]{1,0:T(8,128)(2,1)} %copy-done.20) | copy-start | bytes 12292
  241.3 6.5 %copy-start.23 = (bf16[32,64]{1,0:T(8,128)(2,1)S(1)}, bf16[32,64]{1,0:T(8,128)(2,1)}, u32[]{:S(2)}) copy-start(bf16[32,64]{1,0:T(8,128)(2,1)} %copy-done.22) | copy-start | bytes 12292
  247.8 2.3 copy-start.2

commit v2 on v0

v2 whole, which is shorter than its diff:
```python
import functools
import math
import jax
import jax.numpy as jnp
import numpy as np
from jax import lax
from jax.experimental import pallas as pl
from jax.experimental.pallas import tpu as pltpu
from jax.sharding import PartitionSpec as P

NORM_EPS = 1e-6
ROPE_THETA = 10000.0
MESH = pl.DeviceIdType.MESH
F32 = jnp.float32
BF16 = jnp.bfloat16
VMEM_ALL = 67043328


def rms_norm(values, gain):
    wide = values.astype(F32)
    mean_sq = jnp.mean(wide * wide, axis=-1, keepdims=True)
    return (wide * lax.rsqrt(mean_sq + NORM_EPS) * gain).astype(BF16)


def nt(a, b):
    return lax.dot_general(a, b, (((1,), (1,)), ((), ())), preferred_element_type=F32)


def nn(a, b):
    return jnp.dot(a, b, preferred_element_type=F32)


def silu_mul(gate, up):
    return (jax.nn.silu(gate) * up).astype(BF16)


def attn_kernel(layer, steps, group, *refs):
    n_in = 13 if layer == 0 else 15
    (x, gain, pos, pos_row, freq, g_kv, wq, wdkv, wuk, wuv, wo, lat, rop) = refs[:13]
    part, lat_out, rop_out = refs[n_in:n_in + 3]
    (wqb, wdkvb, wukb, wuvb, wob, latb, ropb, qls, qrs, latn, ropn, outs, wide,
     wsem, csem, osem) = refs[n_in + 3:]
    lora = g_kv.shape[1]
    tok = latb.shape[0]
    cache = latb.shape[1]
    rope = ropb.shape[1]
    half = rope // 2
    heads = outs.shape[1] // (steps * tok)
    qk = wqb.shape[0] // heads
    nope = qk - rope
    scale = 1.0 / math.sqrt(qk)
    per = steps * heads
    n_group = tok // group

    loads = []
    for i, (src, dst) in enumerate(((wq, wqb), (wdkv, wdkvb), (wuk, wukb), (wuv, wuvb), (wo, wob))):
        loads.append(pltpu.make_async_copy(src.at[layer], dst, wsem.at[i]))

    def cache_in(g):
        t = pl.ds(g * group, group)
        return (pltpu.make_async_copy(lat.at[layer, t], latb.at[t], csem.at[0, g]),
                pltpu.make_async_copy(rop.at[layer, t], ropb.at[t], csem.at[1, g]))

    def cache_out(g):
        t = pl.ds(g * group, group)
        return (pltpu.make_async_copy(latb.at[t], lat_out.at[layer, t], osem.at[0, g]),
                pltpu.make_async_copy(ropb.at[t], rop_out.at[layer, t], osem.at[1, g]))

    for cp in loads[:3]:
        cp.start()

    places = jnp.concatenate([pos_row[...] + s for s in range(steps)], axis=1).astype(F32)
    angle = freq[...] * places
    cos_t, sin_t = jnp.cos(angle), jnp.sin(angle)
    first = lax.broadcasted_iota(jnp.int32, angle.shape, 0) < half
    cosf, sinf = jnp.transpose(cos_t), jnp.transpose(jnp.where(first, -sin_t, sin_t))
    cost, sint = cos_t[:half], sin_t[:half]

    normed = rms_norm(x[...], gain[layer:layer + 1, :]) if layer == 0 else x[...]
    loads[0].wait()
    for g in range(n_group):
        for cp in cache_in(g):
            cp.start()
    for cp in loads[3:]:
        cp.start()
    query = nt(normed, wqb[...])
    loads[1].wait()
    kv = nt(normed, wdkvb[:lora, :])
    latn[...] = rms_norm(kv, g_kv[layer:layer + 1, :]).astype(F32)
    key = nt(wdkvb[lora:, :], normed)
    k1, k2 = key[:half], key[half:]
    ropn[...] = jnp.concatenate([k1 * cost - k2 * sint, k2 * cost + k1 * sint], axis=0).astype(BF16).astype(F32)
    loads[2].wait()
    wide[...] = wukb[...].astype(F32)
    for h in range(heads):
        base = h * qk
        qn = query[:, base:base + nope].astype(BF16)
        pe = query[:, base + nope:base + qk]
        swapped = jnp.concatenate([pe[:, half:], pe[:, :half]], axis=1)
        turned = pe * cosf + swapped * sinf
        ql = nt(qn, wide[pl.ds(h, lora, stride=heads), :].astype(BF16))
        for s in range(steps):
            at = slice((s * heads + h) * tok, (s * heads + h + 1) * tok)
            qrs[at, :rope] = turned[s * tok:(s + 1) * tok]
            for c in range(lora // 128):
                qls[c, at, :] = ql[s * tok:(s + 1) * tok, c * 128:(c + 1) * 128]

    row16 = lax.broadcasted_iota(jnp.int32, (16, lora), 0)
    lane_c = lax.broadcasted_iota(jnp.int32, (rope, cache), 1)
    lane_r = lax.broadcasted_iota(jnp.int32, (rope, steps * tok), 1)
    lane_s = lax.broadcasted_iota(jnp.int32, (per, cache), 1)
    step_s = lax.broadcasted_iota(jnp.int32, (per, cache), 0) // heads

    def run_group(g, _):
        for cp in cache_in(g):
            cp.wait()
        for j in range(group):
            b = g * group + j
            p = pos[b]
            rb = ropb[b].astype(F32)
            for s in range(steps):
                slot = p + s
                start = pl.multiple_of((slot // 16) * 16, 16)
                old = latb[b, pl.ds(start, 16), :].astype(F32)
                new = latn[pl.ds(s * tok + b, 1), :]
                latb[b, pl.ds(start, 16), :] = jnp.where(row16 == slot - start, new, old).astype(BF16)
                col = jnp.sum(jnp.where(lane_r == s * tok + b, ropn[...], 0.0), axis=1, keepdims=True)
                rb = jnp.where(lane_c == slot, col, rb)
            ropb[b] = rb.astype(BF16)
        for cp in cache_out(g):
            cp.start()
        probs = []
        for j in range(group):
            b = g * group + j
            mine = pl.ds(b, per, stride=tok)
            ql = jnp.concatenate([qls[c, mine, :] for c in range(lora // 128)], axis=1).astype(BF16)
            qr = qrs[mine, :][:, :rope].astype(BF16)
            sc = (nt(ql, latb[b]) + nn(qr, ropb[b])) * scale
            sc = jnp.where(lane_s <= pos[b] + step_s, sc, -1e30)
            ex = jnp.exp(sc - jnp.max(sc, axis=-1, keepdims=True))
            probs.append((ex / jnp.sum(ex, axis=-1, keepdims=True)).astype(BF16))
        for j in range(group):
            b = g * group + j
            val = nn(probs[j], latb[b])
            for c in range(lora // 128):
                outs[c, pl.ds(b, per, stride=tok), :] = val[:, c * 128:(c + 1) * 128]
        return 0

    lax.fori_loop(0, n_group, run_group, 0)
    loads[3].wait()
    wide[...] = wuvb[...].astype(F32)
    vals = []
    for h in range(heads):
        ol = jnp.concatenate([
            jnp.concatenate([outs[c, (s * heads + h) * tok:(s * heads + h + 1) * tok, :] for s in range(steps)], axis=0)
            for c in range(lora // 128)], axis=1).astype(BF16)
        vals.append(nn(ol, wide[pl.ds(h, lora, stride=heads), :].astype(BF16)).astype(BF16))
    loads[4].wait()
    part[...] = nn(jnp.concatenate(vals, axis=1), wob[...])
    for g in range(n_group):
        for cp in cache_out(g):
            cp.wait()


def attention(layer, steps, x, gain, pos, freq, g_kv, wq, wdkv, wuk, wuv, wo, lat, rop, outs):
    rows = x.shape[0]
    tok, cache, lora = lat.shape[1:]
    rope = rop.shape[2]
    hidden = wo.shape[2]
    heads = wq.shape[1]
    qk = wq.shape[2]
    group = 8
    vm = pl.BlockSpec(memory_space=pltpu.VMEM)
    hbm = pl.BlockSpec(memory_space=pl.ANY)
    sm = pl.BlockSpec(memory_space=pltpu.SMEM)
    wq2 = wq.reshape(wq.shape[0], heads * qk, -1)
    args = [x, gain, pos, pos[None, :], freq, g_kv, wq2, wdkv, wuk, wuv, wo, lat, rop]
    specs = [vm, vm, sm] + [vm] * 3 + [hbm] * 7
    alias = {}
    if outs is not None:
        args += list(outs)
        specs += [hbm, hbm]
        alias = {13: 1, 14: 2}
    dma = pltpu.SemaphoreType.DMA
    return pl.pallas_call(
        functools.partial(attn_kernel, layer, steps, group),
        out_shape=[jax.ShapeDtypeStruct((rows, hidden), F32),
                   jax.ShapeDtypeStruct(lat.shape, BF16), jax.ShapeDtypeStruct(rop.shape, BF16)],
        in_specs=specs,
        out_specs=[vm, hbm, hbm],
        input_output_aliases=alias,
        scratch_shapes=[
            pltpu.VMEM(wq2.shape[1:], BF16), pltpu.VMEM(wdkv.shape[1:], BF16), pltpu.VMEM(wuk.shape[1:], BF16),
            pltpu.VMEM(wuv.shape[1:], BF16), pltpu.VMEM(wo.shape[1:], BF16),
            pltpu.VMEM((tok, cache, lora), BF16), pltpu.VMEM((tok, rope, cache), BF16),
            pltpu.VMEM((lora // 128, rows * heads, 128), F32), pltpu.VMEM((rows * heads, 128), F32),
            pltpu.VMEM((rows, lora), F32), pltpu.VMEM((rope, rows), F32), pltpu.VMEM((lora // 128, rows * heads, 128), F32),
            pltpu.VMEM(wuk.shape[1:], F32),
            dma((5,)), dma((2, tok // group)), dma((2, tok // group)),
        ],
        compiler_params=pltpu.CompilerParams(vmem_limit_bytes=VMEM_ALL),
        name="attn%d" % layer,
    )(*args)


def remote(src, dst, send, recv, where):
    return pltpu.make_async_remote_copy(src_ref=src, dst_ref=dst, send_sem=send, recv_sem=recv,
                                        device_id=where, device_id_type=MESH)


def turn(me, d, n):
    return lax.rem(me + d, n)


def fetch(refs, sem):
    half = len(refs) // 2
    cps = [pltpu.make_async_copy(src, dst, sem.at[i]) for i, (src, dst) in enumerate(zip(refs[:half], refs[half:]))]
    for cp in cps:
        cp.start()
    return cps, refs[half:]


def rows_reduce(part, bufs, sems, me, n_tp, rows):
    relay, fin = bufs
    hidden = part.shape[1]
    lo, hi = pl.ds(0, hidden // 2), pl.ds(hidden // 2, hidden // 2)
    up, far, down = turn(me, 1, n_tp), turn(me, 2, n_tp), turn(me, n_tp - 1, n_tp)

    def at(owner):
        return pl.ds(owner * rows, rows)

    def send(src, dst, i, peer):
        cp = remote(src, dst, sems[0].at[i], sems[1].at[i], {"tp": peer})
        cp.start()
        return cp

    cps = [send(part.at[at(far), lo], relay.at[0], 0, up), send(part.at[at(far), hi], relay.at[1], 1, down),
           send(part.at[at(up), hi], fin.at[0, :, hi], 2, up), send(part.at[at(down), lo], fin.at[1, :, lo], 3, down)]
    cps[0].wait_recv()
    relay[0] = relay[0] + part[at(up), lo]
    cps.append(send(relay.at[0], fin.at[0, :, lo], 4, up))
    cps[1].wait_recv()
    relay[1] = relay[1] + part[at(down), hi]
    cps.append(send(relay.at[1], fin.at[1, :, hi], 5, down))
    for cp in cps[2:]:
        cp.wait_recv()
    return part[at(me), :] + (fin[0] + fin[1]), cps


def reduce_scratch(own, hidden):
    return [pltpu.VMEM((2, own, hidden // 2), F32), pltpu.VMEM((2, own, hidden), F32)]


def rows_gather(buf, s, r, me, n_tp):
    cps = []
    for d in range(1, n_tp):
        cp = remote(buf.at[me], buf.at[me], s.at[d - 1], r.at[d - 1], {"tp": turn(me, d, n_tp)})
        cp.start()
        cps.append(cp)
    return cps


def mid_kernel(n_tp, n_ep, step, part_in, resid_in, gain0_in, gain1_in, ids_in, wg, wu, wd,
               own_out, norm_out, ids_out, part, resid, gain0, gain1, ids, in_sem,
               wgb, wub, wdb, relay0, recv0, relay1, recv1, gath0, gath1, acc, ids_own, ids_all,
               wsem, s1, r1, s2, r2, s3, r3, s4, r4, s5, r5):
    me = lax.axis_index("tp")
    ep = lax.axis_index("ep")
    total_rows, hidden = part.shape
    rows = total_rows // n_tp
    first, _ = fetch((part_in, resid_in, gain0_in, gain1_in, ids_in, part, resid, gain0, gain1, ids), in_sem)
    barrier = pltpu.get_barrier_semaphore()
    for d in range(1, n_tp):
        pl.semaphore_signal(barrier, inc=1, device_id={"tp": turn(me, d, n_tp)}, device_id_type=MESH)
    for d in range(1, n_ep):
        pl.semaphore_signal(barrier, inc=1, device_id={"ep": turn(ep, d, n_ep)}, device_id_type=MESH)
    pl.semaphore_wait(barrier, n_tp - 1 + n_ep - 1)
    for cp in first:
        cp.wait()
    loads = []
    for i, (src, dst) in enumerate(((wg, wgb), (wu, wub), (wd, wdb))):
        cp = pltpu.make_async_copy(src, dst, wsem.at[i])
        cp.start()
        loads.append(cp)

    id_cps = []
    picks = jnp.concatenate([ids[:, i, :] for i in range(ids.shape[1])], axis=1).astype(F32)
    picks = jnp.concatenate([picks, jnp.zeros((8 - picks.shape[0], picks.shape[1]), F32)], axis=0)
    ids_own[...] = jnp.zeros(ids_own.shape, jnp.int32)
    ids_own[:, 0:8] = jnp.transpose(picks).astype(jnp.int32)
    for d in range(1, n_ep):
        cp = remote(ids_own, ids_all.at[ep], s5.at[d - 1], r5.at[d - 1], {"ep": turn(ep, d, n_ep)})
        cp.start()
        id_cps.append(cp)
    ids_out[ep] = ids_own[...]
    own = pl.ds(me * rows, rows)
    total, red0 = rows_reduce(part, (relay0, recv0), (s1, r1), me, n_tp, rows)
    y = (resid[own, :].astype(F32) + total).astype(BF16)
    gath0[me] = rms_norm(y, gain0[0:1, :])
    gat0 = rows_gather(gath0, s2, r2, me, n_tp)
    for cp in loads:
        cp.wait()
    for cp in gat0:
        cp.wait_recv()

    width = wgb.shape[0]

    def chunk(start, size, first):
        x = gath0[...].reshape(total_rows, hidden)
        act = silu_mul(nt(x, wgb[pl.ds(start, size), :]), nt(x, wub[pl.ds(start, size), :]))
        down = nn(act, wdb[pl.ds(start, size), :])
        acc[...] = down if first else acc[...] + down

    whole = width // step
    chunk(0, step, True)

    def body(i, _):
        chunk(pl.multiple_of(i * step, step), step, False)
        return 0

    lax.fori_loop(1, whole, body, 0)
    if width % step:
        chunk(whole * step, width % step, False)

    total, red1 = rows_reduce(acc, (relay1, recv1), (s3, r3), me, n_tp, rows)
    h = (y.astype(F32) + total).astype(BF16)
    own_out[...] = h
    normed = rms_norm(h, gain1[1:2, :])
    gath1[me] = normed
    gat1 = rows_gather(gath1, s4, r4, me, n_tp)
    norm_out[own, :] = normed
    for d in range(1, n_ep):
        id_cps[d - 1].wait_recv()
        src = turn(ep, n_ep - d, n_ep)
        ids_out[src] = ids_all[src]
    for d in range(1, n_tp):
        gat1[d - 1].wait_recv()
        src = turn(me, n_tp - d, n_tp)
        norm_out[pl.ds(src * rows, rows), :] = gath1[src]
    for cp in red0 + gat0 + red1 + gat1 + id_cps:
        cp.wait_send()


def mid(n_tp, n_ep, part, resid, gain0, gain1, ids, wg, wu, wd):
    rows, hidden = part.shape
    first = (part, resid, gain0, gain1, ids)
    own = rows // n_tp
    dma = pltpu.SemaphoreType.DMA
    vm = pl.BlockSpec(memory_space=pltpu.VMEM)
    hbm = pl.BlockSpec(memory_space=pl.ANY)
    return pl.pallas_call(
        functools.partial(mid_kernel, n_tp, n_ep, 512),
        out_shape=[jax.ShapeDtypeStruct((own, hidden), BF16), jax.ShapeDtypeStruct((rows, hidden), BF16),
                   jax.ShapeDtypeStruct((n_ep, rows, 128), ids.dtype)],
        in_specs=[hbm] * 8,
        out_specs=[vm] * 3,
        scratch_shapes=[
            *[pltpu.VMEM(v.shape, v.dtype) for v in first], dma((len(first),)),
            pltpu.VMEM(wg.shape, BF16), pltpu.VMEM(wu.shape, BF16), pltpu.VMEM(wd.shape, BF16),
            *reduce_scratch(own, hidden), *reduce_scratch(own, hidden),
            pltpu.VMEM((n_tp, own, hidden), BF16), pltpu.VMEM((n_tp, own, hidden), BF16),
            pltpu.VMEM((rows, hidden), F32), pltpu.VMEM((rows, 128), ids.dtype), pltpu.VMEM((n_ep, rows, 128), ids.dtype),
            dma((3,))] + [dma((6,)), dma((6,)), dma((n_tp - 1,)), dma((n_tp - 1,))] * 2 + [dma((n_ep - 1,))] * 2,
        compiler_params=pltpu.CompilerParams(collective_id=0, has_side_effects=True, vmem_limit_bytes=VMEM_ALL),
        name="mid",
    )(*first, wg, wu, wd)


def moe_kernel(n_tp, n_ep, top_k, part_in, resid_in, gain_in, router_in, ids_in, sg, su, sd, eg, eu, ed, out,
               part, resid, gain, router, ids, in_sem,
               wg, wu, wd, vg, vu, vd, xs, y_own, relay0, recv0, comb, acc, drecv, xrelay, xrecv, shbuf, xpair, acts,
               relay1, recv1, obuf,
               wsem, vsem, s1, r1, sx, rx, sy, ry, sz, rz, sd2, rd2, sa, ra, sb, rb, sc, rc, so, ro):
    me = lax.axis_index("tp")
    ep = lax.axis_index("ep")
    xi, core = ep // 2, lax.rem(ep, 2)
    n_x = n_ep // 2
    partner = ep + 1 - 2 * core
    rows = part.shape[0] // n_tp
    hidden = part.shape[1]
    block = part.shape[0]
    n_exp = wg.shape[0]
    lo, hi = pl.ds(0, hidden // 2), pl.ds(hidden // 2, hidden // 2)
    up, down = turn(me, 1, n_tp), turn(me, n_tp - 1, n_tp)

    start, _ = fetch((part_in, resid_in, gain_in, router_in, ids_in, part, resid, gain, router, ids), in_sem)
    barrier = pltpu.get_barrier_semaphore()
    for d in range(1, n_tp):
        pl.semaphore_signal(barrier, inc=1, device_id={"tp": turn(me, d, n_tp)}, device_id_type=MESH)
    for d in range(1, n_x):
        pl.semaphore_signal(barrier, inc=1, device_id={"ep": turn(ep, 2 * d, n_ep)}, device_id_type=MESH)
    pl.semaphore_signal(barrier, inc=1, device_id={"ep": partner}, device_id_type=MESH)
    pl.semaphore_wait(barrier, n_tp + n_x - 1)
    for cp in start:
        cp.wait()
    loads = []
    for i, (src, dst) in enumerate(((sg, vg), (su, vu), (sd, vd))):
        cp = pltpu.make_async_copy(src, dst, vsem.at[i])
        cp.start()
        loads.append(cp)
    for e in range(n_exp):
        for i, (src, dst) in enumerate(((eg, wg), (eu, wu), (ed, wd))):
            pltpu.make_async_copy(src.at[e], dst.at[e], wsem.at[i, e]).start()


    total, pend = rows_reduce(part, (relay0, recv0), (s1, r1), me, n_tp, rows)
    y = (resid[...].astype(F32) + total).astype(BF16)
    y_own[...] = y
    xs[ep, me] = rms_norm(y, gain[1:2, :])

    order = [2, 1, 3, 0]
    source = [turn(ep, n_ep - 2 * k, n_ep) for k in range(n_x)]
    xcp, ycp, zcp, pcp = {}, {}, {}, {}
    for k in order[:-1]:
        xcp[k] = remote(xs.at[ep, me], xs.at[ep, me], sx.at[k - 1], rx.at[k - 1], {"ep": turn(ep, 2 * k, n_ep)})
        xcp[k].start()
    far = turn(me, 2, n_tp)
    for k in [0] + order[:-1]:
        if k:
            xcp[k].wait_recv()
        mine = xs.at[source[k], me]
        for i, peer in enumerate((up, down, far) if k == order[0] else (up, down)):
            ycp[k, i] = remote(mine, mine, sy.at[k, i], ry.at[k, i], {"tp": peer})
            ycp[k, i].start()

    def forward(k):
        for i, (origin, peer, part_of) in enumerate(((down, up, lo), (up, down, hi))):
            ycp[k, i].wait_recv()
            piece = xs.at[source[k], origin, :, part_of]
            zcp[k, i] = remote(piece, piece, sz.at[k, i], rz.at[k, i], {"tp": peer})
            zcp[k, i].start()

    def across(k):
        for i in range(2 if k != order[0] else 3):
            (zcp if k != order[0] else ycp)[k, i].wait_recv()
        pcp[k] = remote(xs.at[source[k]], xs.at[source[k]], sd2.at[k], rd2.at[k], {"ep": partner})
        pcp[k].start()

    acc[...] = jnp.zeros(acc.shape, F32)
    forward(0)
    across(0)
    for cp in loads:
        cp.wait()
    own = xs[ep].reshape(block, hidden)
    shbuf[...] = nn(silu_mul(nt(own, vg[...]), nt(own, vu[...])), vd[...])
    across(order[0])

    def weights(at, x, xb):
        logits = nt(x, router[...])
        ex = jnp.exp(logits - jnp.max(logits, axis=-1, keepdims=True))
        prob = ex / jnp.sum(ex, axis=-1, keepdims=True)
        lane = lax.broadcasted_iota(jnp.int32, prob.shape, 1)
        picks = ids[pl.ds(2 * xb, 2)].reshape(2 * block, ids.shape[-1])
        chosen = lane == picks[:, 0:1]
        for j in range(1, top_k):
            chosen = chosen | (lane == picks[:, j:j + 1])
        comb[at] = jnp.where(chosen, prob, 0.0)

    half = hidden // 2
    pieces = (lo, hi)

    def gate_up(xk, e, first=False):
        if first:
            for i, (src, dst) in enumerate(((eg, wg), (eu, wu), (ed, wd))):
                pltpu.make_async_copy(src.at[e], dst.at[e], wsem.at[i, e]).wait()
        return jnp.transpose(jax.nn.silu(nt(wg[e], xk)) * nt(wu[e], xk)).astype(BF16)

    def add_down(act, e, at, count, piece):
        n = 2 * block * count
        cw = comb[at:at + count].reshape(n, comb.shape[-1])
        lane = lax.broadcasted_iota(jnp.int32, cw.shape, 1)
        col = jnp.sum(jnp.where(lane == ep * n_exp + e, cw, 0.0), axis=-1, keepdims=True)
        for q in range(2):
            cs = pl.ds(piece * half + q * (half // 2), half // 2)
            acc[at:at + count, :, cs] += (col * nn(act, wd[e, :, cs])).reshape(count, 2 * block, half // 2)

    def experts(load, at, lo_e, hi_e, first=False):
        def body(e, _):
            act = gate_up(load(), e, first)
            for piece in range(2):
                add_down(act, e, at, 1, piece)
            return 0
        lax.fori_loop(lo_e, hi_e, body, 0)

    def pair_acts(lo_e, hi_e):
        def body(e, _):
            acts[e] = gate_up(xpair[...], e)
            return 0
        lax.fori_loop(lo_e, hi_e, body, 0)

    def pair_down(piece, lo_e, hi_e):
        def body(e, _):
            add_down(acts[e], e, 1, 2, piece)
            return 0
        lax.fori_loop(lo_e, hi_e, body, 0)

    target = [turn(xi, d, n_x) for d in (2, 1, n_x - 1, 0)]
    arrive = [2, n_x - 1, 1, 0]
    kept = pl.ds(core * block, block)
    other = pl.ds((1 - core) * block, block)
    dcp, acp = {}, {}

    def ready(b):
        pcp[arrive[b]].wait_recv()

    def cross(b, piece):
        cs = pieces[piece]
        dcp[b, piece] = remote(acc.at[b, other, cs], drecv.at[b, :, cs], sb.at[b, piece], rb.at[b, piece], {"ep": partner})
        dcp[b, piece].start()

    def along(src, dst, i, d):
        acp[i] = remote(src, dst, sa.at[i], ra.at[i], {"ep": turn(ep, 2 * d, n_ep)})
        acp[i].start()

    def settle(b, piece):
        cs = pieces[piece]
        dcp[b, piece].wait_recv()
        drecv[b, :, cs] = drecv[b, :, cs] + acc[b, kept, cs]

    def pass_on(piece):
        for b, d in ((1, 1), (2, n_x - 1)):
            cs = pieces[piece]
            settle(b, piece)
            if b == piece + 1:
                acp[piece].wait_recv()
                drecv[b, :, cs] = drecv[b, :, cs] + xrelay[piece]
            along(drecv.at[b, :, cs], xrecv.at[b - 1, :, cs], 2 * b + piece, d)

    ready(0)
    far_rows = lambda: xs[pl.ds(2 * target[0], 2)].reshape(2 * block, hidden)
    weights(0, far_rows(), target[0])
    experts(far_rows, 0, 0, 2, True)
    forward(1)
    forward(3)
    experts(far_rows, 0, 2, 5, True)
    across(1)
    across(3)
    experts(far_rows, 0, 5, n_exp, True)
    for piece in range(2):
        cross(0, piece)
    for b in (1, 2):
        ready(b)
        xb = xs[pl.ds(2 * target[b], 2)].reshape(2 * block, hidden)
        xpair[(b - 1) * 2 * block:b * 2 * block, :] = xb
        weights(b, xb, target[b])
    pair_acts(0, 1)
    for piece in range(2):
        settle(0, piece)
        along(drecv.at[0, :, pieces[piece]], xrelay.at[piece], piece, (1, n_x - 1)[piece])
    pair_acts(1, n_exp)
    pair_down(0, 0, n_exp)
    for b in (1, 2):
        cross(b, 0)
    pair_down(1, 0, n_exp // 2)
    pass_on(0)
    pair_down(1, n_exp // 2, n_exp)
    for b in (1, 2):
        cross(b, 1)
    ready(3)
    own_rows = lambda: xs[pl.ds(2 * target[3], 2)].reshape(2 * block, hidden)
    weights(3, own_rows(), target[3])
    experts(own_rows, 3, 0, 2)
    pass_on(1)
    experts(own_rows, 3, 2, n_exp)
    for piece in range(2):
        cross(3, piece)
    for piece in range(2):
        settle(3, piece)
    for i in range(2, 6):
        acp[i].wait_recv()
    drecv[3] = drecv[3] + shbuf[...] + (xrecv[0] + xrecv[1])
    total, last = rows_reduce(drecv.at[3], (relay1, recv1), (sc, rc), me, n_tp, rows)
    fin = (y_own[...].astype(F32) + total).astype(BF16)
    obuf[me] = fin
    ocp = rows_gather(obuf, so, ro, me, n_tp)
    out[pl.ds(me * rows, rows), :] = fin
    for d in range(1, n_tp):
        ocp[d - 1].wait_recv()
        src = turn(me, n_tp - d, n_tp)
        out[pl.ds(src * rows, rows), :] = obuf[src]
    pend = pend + list(xcp.values()) + list(ycp.values()) + list(zcp.values()) + list(pcp.values())
    for cp in pend + list(dcp.values()) + list(acp.values()) + last + ocp:
        cp.wait_send()


def moe(n_tp, n_ep, top_k, part, resid, gain, router, ids, sg, su, sd, eg, eu, ed):
    rows, hidden = part.shape
    own = rows // n_tp
    n_x = n_ep // 2
    dma = pltpu.SemaphoreType.DMA
    n_exp = eg.shape[0]
    vm = pl.BlockSpec(memory_space=pltpu.VMEM)
    hbm = pl.BlockSpec(memory_space=pl.ANY)
    first = (part, resid, gain, router, ids)
    scratch = [
        *[pltpu.VMEM(v.shape, v.dtype) for v in first], dma((len(first),)),
        pltpu.VMEM(eg.shape, BF16), pltpu.VMEM(eu.shape, BF16), pltpu.VMEM(ed.shape, BF16),
        pltpu.VMEM(sg.shape, BF16), pltpu.VMEM(su.shape, BF16), pltpu.VMEM(sd.shape, BF16),
        pltpu.VMEM((n_ep, n_tp, own, hidden), BF16),
        pltpu.VMEM((own, hidden), BF16),
        *reduce_scratch(own, hidden),
        pltpu.VMEM((n_x, 2 * rows, router.shape[0]), F32),
        pltpu.VMEM((n_x, 2 * rows, hidden), F32),
        pltpu.VMEM((n_x, rows, hidden), F32),
        pltpu.VMEM((2, rows, hidden // 2), F32),
        pltpu.VMEM((2, rows, hidden), F32),
        pltpu.VMEM((rows, hidden), F32),
        pltpu.VMEM((4 * rows, hidden), BF16),
        pltpu.VMEM((n_exp, 4 * rows, eg.shape[1]), BF16),
        *reduce_scratch(own, hidden),
        pltpu.VMEM((n_tp, own, hidden), BF16),
        dma((3, n_exp)), dma((3,)),
        *[dma((6,))] * 2, *[dma((n_x - 1,))] * 2, *[dma((n_x, 3))] * 2, *[dma((n_x, 2))] * 2, *[dma((n_x,))] * 2,
        *[dma((6,))] * 2, *[dma((n_x, 2))] * 2, *[dma((6,))] * 2,
        dma((n_tp - 1,)), dma((n_tp - 1,)),
    ]
    return pl.pallas_call(
        functools.partial(moe_kernel, n_tp, n_ep, top_k),
        out_shape=jax.ShapeDtypeStruct((rows, hidden), BF16),
        in_specs=[hbm] * 11,
        out_specs=vm,
        scratch_shapes=scratch,
        compiler_params=pltpu.CompilerParams(collective_id=2, has_side_effects=True, vmem_limit_bytes=VMEM_ALL),
        name="moe",
    )(*first, sg, su, sd, eg, eu, ed)


def solution(mesh):
    tok_axes = ('dp', 'ep')
    n_tp, n_ep = mesh.shape['tp'], mesh.shape['ep']

    def device_fn(emb, pos, route_ids, lat_cache, rope_cache, attn_norm, w_q, w_dkv, kv_norm, w_uk, w_uv, w_o, mlp_norm, dense_gate, dense_up, dense_down, router, shared_gate, shared_up, shared_down, expert_gate, expert_up, expert_down):
        steps, tokens, hidden = emb.shape
        rows = steps * tokens
        emb_rows = emb.reshape(rows, hidden)
        ids = route_ids.transpose(2, 0, 1)
        rope_dim = rope_cache.shape[-1]
        inv_freq = np.float32(ROPE_THETA) ** (-(np.arange(rope_dim // 2, dtype=np.float32) * np.float32(2.0) / np.float32(rope_dim)))
        freq = jnp.asarray(np.concatenate([inv_freq, inv_freq])[:, None])
        layers = w_q.shape[0]
        wq_t = w_q.transpose(0, 2, 3, 1)
        wdkv_t = w_dkv.swapaxes(1, 2)
        rop_t = rope_cache.swapaxes(2, 3)
        wuk = w_uk.reshape(layers, -1, w_uk.shape[-1])
        wuv = w_uv.reshape(layers, -1, w_uv.shape[-1])

        def attend(layer, x, outs):
            return attention(layer, steps, x, attn_norm, pos, freq, kv_norm, wq_t, wdkv_t, wuk, wuv, w_o, lat_cache, rop_t, outs)

        part, *outs = attend(0, emb_rows, None)
        h_own, normed, ids_all = mid(n_tp, n_ep, part, emb_rows, mlp_norm, attn_norm, ids, dense_gate.T, dense_up.T, dense_down)
        part, lat_out, rop_out = attend(1, normed, outs)
        out = moe(n_tp, n_ep, route_ids.shape[-1], part, h_own, mlp_norm, router.T, ids_all, shared_gate.T, shared_up.T, shared_down, expert_gate.swapaxes(1, 2), expert_up.swapaxes(1, 2), expert_down)
        return out.reshape(steps, tokens, hidden), lat_out, rop_out.swapaxes(2, 3)

    tok, wide, tall = P(None, tok_axes), P(None, 'tp'), P('tp')
    heads = P(None, None, 'tp')
    in_specs = (tok, P(tok_axes), tok, tok, tok, P(), heads, P(), P(), heads, heads, wide, P(), wide, wide, tall, P(), wide, wide, tall, P('ep', None, 'tp'), P('ep', None, 'tp'), P('ep', 'tp'))
    out_specs = (tok, tok, tok)
    return jax.shard_map(device_fn, mesh=mesh, in_specs=in_specs, out_specs=out_specs, check_vma=False)
```

time: 635 us -> 148 us (0.23); the launches traced: 625 us -> 148 us
  other arithmetic: 121 us -> 0 us
  matrix products: 120 us -> 0 us
  waiting for transfers between devices: 120 us -> 0 us
  local copies, waits for them, and re-layouts: 114 us -> 1.67 us
  Pallas kernels: 34.6 us -> 146 us
  blocking collectives: 97.8 us -> 0 us
  between operations: 15.8 us -> 0.66 us
    pallas_call x0 -> x4, Pallas kernels: none -> 146 us  [the longest x1 80.5 us: moe(): pl.pallas_call(functools.partial(moe_kernel, n_tp, n_ep, top_k), out_shap...]
    dot_general x38 -> x0, matrix products: 111 us -> none  [the longest x4 36 us: swiglu(): return jnp.dot(act_bf, w_down, preferred_element_type=jnp.float32)]
    all_gather x4 -> x0, blocking collectives: 97.8 us -> none  [the longest x2 52.7 us: routed_local(): weight_all = lax.all_gather(route_w, 'ep', axis=0, tiled=True)]
    psum x4 -> x0, waiting for transfers between devices: 95.5 us -> none  [the longest x2 37.9 us: device_fn(): lax.psum(attn_part, 'tp')]
    gather x16 -> x0, local copies, waits for them, and re-layouts: 71.1 us -> none  [the longest x2 28.1 us: routed_local(): sorted_rows = jnp.take(tok_all, tok_index, axis=0)]
    scatter-add x2 -> x0, other arithmetic: 47.3 us -> none  [routed_local(): jax.ops.segment_sum(contrib, tok_index, num_segments=tok_all.shape[0])]
    another operation x6 -> x0, Pallas kernels: 31.6 us -> none
    unnamed x172 -> x1, local copies, waits for them, and re-layouts: 32 us -> 1.67 us
  transfers between devices with their start and end apart: 8 -> 0, of which waited for: 4 -> 0; matrix products, arithmetic and copies ran while one was open for 36% -> 0% of each run, Pallas kernels for 6% -> 0%
where the time goes in v2:
time: 148 us
  Pallas kernels  146 us (99%)
  local copies, waits for them, and re-layouts  1.67 us (1%)
    pallas_call x1, Pallas kernels, moe(): pl.pallas_call(functools.partial(moe_kernel, n_tp, n_ep, top_k), out_shap...  80.5 us
    pallas_call x1, Pallas kernels, mid(): pl.pallas_call(functools.partial(mid_kernel, n_tp, n_ep, 512), out_shape=...  43.5 us
    pallas_call x2, Pallas kernels, attention(): pl.pallas_call(functools.partial(attn_kernel, layer, steps, group), out_s...  22 us

profile of v2, /device:TPU:96, one launch (start us, length us, event | category | flops | bytes accessed | tf_op | source)
XLA Modules:
  0.0 148.3 jit_solution(12666899182389968114)
XLA Ops:
  0.6 11.0 %attn0.1 = (f32[64,2048]{1,0:T(8,128)}, bf16[2,32,128,512]{3,2,1,0:T(8,128)(2,1)}, bf16[2,32,64,128]{3,2,1,0:T(8,128)(2,1)}) custom-call(bf16[64,2048]{1,0:T(8,128)(2,1)} %bitcast.35, f32[2,2048]{1,0:T(2,128)} %refs_1_.3, s32[32]{0:T(128)} %refs_2_.3, s32[1,32]{1,0:T(1,128)} %bitcast.40, f32[64,1]{1,0:T(8,128)} %constant.2.clone.refs_4_, f32[2,512]{1,0:T(2,128)} %refs_5_.3, ...), custom_call_target="tpu_custom_call" | custom-call | tf_op jit(solution)/shard_map/attn0/pallas_call | solution.py:185
  11.7 43.5 %mid.1 = (bf16[16,2048]{1,0:T(8,128)(2,1)}, bf16[64,2048]{1,0:T(8,128)(2,1)}, s32[8,64,128]{2,1,0:T(8,128)}) custom-call(f32[64,2048]{1,0:T(8,128)} %get-tuple-element.12.part_in, bf16[64,2048]{1,0:T(8,128)(2,1)} %bitcast.36, f32[2,2048]{1,0:T(2,128)} %gain_in.1, f32[2,2048]{1,0:T(2,128)} %refs_1_.3, s32[6,2,32]{2,1,0:T(2,128)} %bitcast.42, ...), custom_call_target="tpu_custom_call" | custom-call | tf_op jit(solution)/shard_map/mid/pallas_call | solution.py:351
  55.1 11.0 %attn1.1 = (f32[64,2048]{1,0:T(8,128)}, bf16[2,32,128,512]{3,2,1,0:T(8,128)(2,1)}, bf16[2,32,64,128]{3,2,1,0:T(8,128)(2,1)}) custom-call(bf16[64,2048]{1,0:T(8,128)(2,1)} %get-tuple-element.13.refs_0_, f32[2,2048]{1,0:T(2,128)} %refs_1_.3, s32[32]{0:T(128)} %refs_2_.3, s32[1,32]{1,0:T(1,128)} %bitcast.41, ...), custom_call_target="tpu_custom_call", output_to_operand_aliasing={{1}: (13, {}), {2}: (14, {})} | custom-call | tf_op jit(solution)/shard_map/attn1/pallas_call | solution.py:185
  66.2 80.5 %moe.1 = bf16[64,2048]{1,0:T(8,128)(2,1)} custom-call(f32[64,2048]{1,0:T(8,128)} %get-tuple-element.16.part_in, bf16[16,2048]{1,0:T(8,128)(2,1)} %get-tuple-element.17.resid_in, f32[2,2048]{1,0:T(2,128)} %gain_in.1, bf16[64,2048]{1,0:T(8,128)(2,1)} %bitcast.39, s32[8,64,128]{2,1,0:T(8,128)} %get-tuple-element.18.ids_in, bf16[704,2048]{1,0:T(8,128)(2,1)} %bitcast.33, ...), custom_call_target="tpu_custom_call" | custom-call | tf_op jit(solution)/shard_map/moe/pallas_call | solution.py:617
  146.7 1.7 %copy.32 = bf16[2,32,2048]{2,1,0:T(8,128)(2,1)} copy(bf16[2,32,2048]{2,1,0:T(8,128)(2,1)} %bitcast.37) | data formatting | bytes 524288

commit v3 on v2

--- a/solution.py
+++ b/solution.py
@@ -252,11 +252,9 @@
 
 
 def rows_gather(buf, s, r, me, n_tp):
-    cps = []
-    for d in range(1, n_tp):
-        cp = remote(buf.at[me], buf.at[me], s.at[d - 1], r.at[d - 1], {"tp": turn(me, d, n_tp)})
-        cp.start()
-        cps.append(cp)
+    cps = [remote(buf.at[me], buf.at[me], s.at[d - 1], r.at[d - 1], {"tp": turn(me, d, n_tp)}) for d in range(1, n_tp)]
+    for cp in cps[1:] + cps[:1]:
+        cp.start()
     return cps
 
 
@@ -419,7 +417,7 @@
         if k:
             xcp[k].wait_recv()
         mine = xs.at[source[k], me]
-        for i, peer in enumerate((up, down, far) if k == order[0] else (up, down)):
+        for i, peer in ((2, far), (0, up), (1, down))[0 if k == order[0] else 1:]:
             ycp[k, i] = remote(mine, mine, sy.at[k, i], ry.at[k, i], {"tp": peer})
             ycp[k, i].start()
 

time: 148 us -> 147 us (level)
  no operation moved by 1% of the time
where the time goes in v3:
time: 147 us
  Pallas kernels  145 us (99%)
  local copies, waits for them, and re-layouts  1.67 us (1%)
    pallas_call x1, Pallas kernels, moe(): pl.pallas_call(functools.partial(moe_kernel, n_tp, n_ep, top_k), out_shap...  79.8 us
    pallas_call x1, Pallas kernels, mid(): pl.pallas_call(functools.partial(mid_kernel, n_tp, n_ep, 512), out_shape=...  42.9 us
    pallas_call x2, Pallas kernels, attention(): pl.pallas_call(functools.partial(attn_kernel, layer, steps, group), out_s...  22 us

profile of v3, /device:TPU:96, one launch (start us, length us, event | category | flops | bytes accessed | tf_op | source)
XLA Modules:
  0.0 147.1 jit_solution(7753058584083044320)
XLA Ops:
  0.6 11.0 %attn0.1 = (f32[64,2048]{1,0:T(8,128)}, bf16[2,32,128,512]{3,2,1,0:T(8,128)(2,1)}, bf16[2,32,64,128]{3,2,1,0:T(8,128)(2,1)}) custom-call(bf16[64,2048]{1,0:T(8,128)(2,1)} %bitcast.35, f32[2,2048]{1,0:T(2,128)} %refs_1_.3, s32[32]{0:T(128)} %refs_2_.3, s32[1,32]{1,0:T(1,128)} %bitcast.40, f32[64,1]{1,0:T(8,128)} %constant.2.clone.refs_4_, f32[2,512]{1,0:T(2,128)} %refs_5_.3, ...), custom_call_target="tpu_custom_call" | custom-call | tf_op jit(solution)/shard_map/attn0/pallas_call | solution.py:185
  11.7 42.9 %mid.1 = (bf16[16,2048]{1,0:T(8,128)(2,1)}, bf16[64,2048]{1,0:T(8,128)(2,1)}, s32[8,64,128]{2,1,0:T(8,128)}) custom-call(f32[64,2048]{1,0:T(8,128)} %get-tuple-element.12.part_in, bf16[64,2048]{1,0:T(8,128)(2,1)} %bitcast.36, f32[2,2048]{1,0:T(2,128)} %gain_in.1, f32[2,2048]{1,0:T(2,128)} %refs_1_.3, s32[6,2,32]{2,1,0:T(2,128)} %bitcast.42, ...), custom_call_target="tpu_custom_call" | custom-call | tf_op jit(solution)/shard_map/mid/pallas_call | solution.py:349
  54.5 11.0 %attn1.1 = (f32[64,2048]{1,0:T(8,128)}, bf16[2,32,128,512]{3,2,1,0:T(8,128)(2,1)}, bf16[2,32,64,128]{3,2,1,0:T(8,128)(2,1)}) custom-call(bf16[64,2048]{1,0:T(8,128)(2,1)} %get-tuple-element.13.refs_0_, f32[2,2048]{1,0:T(2,128)} %refs_1_.3, s32[32]{0:T(128)} %refs_2_.3, s32[1,32]{1,0:T(1,128)} %bitcast.41, ...), custom_call_target="tpu_custom_call", output_to_operand_aliasing={{1}: (13, {}), {2}: (14, {})} | custom-call | tf_op jit(solution)/shard_map/attn1/pallas_call | solution.py:185
  65.6 79.8 %moe.1 = bf16[64,2048]{1,0:T(8,128)(2,1)} custom-call(f32[64,2048]{1,0:T(8,128)} %get-tuple-element.16.part_in, bf16[16,2048]{1,0:T(8,128)(2,1)} %get-tuple-element.17.resid_in, f32[2,2048]{1,0:T(2,128)} %gain_in.1, bf16[64,2048]{1,0:T(8,128)(2,1)} %bitcast.39, s32[8,64,128]{2,1,0:T(8,128)} %get-tuple-element.18.ids_in, bf16[704,2048]{1,0:T(8,128)(2,1)} %bitcast.33, ...), custom_call_target="tpu_custom_call" | custom-call | tf_op jit(solution)/shard_map/moe/pallas_call | solution.py:615
  145.4 1.7 %copy.32 = bf16[2,32,2048]{2,1,0:T(8,128)(2,1)} copy(bf16[2,32,2048]{2,1,0:T(8,128)(2,1)} %bitcast.37) | data formatting | bytes 524288
